TPU v7x, 32 devices: a 4x4x1 block of a 4x4x8 slice. The times are simulated.
32 devices in a mesh: rhs: 1 (over z), mode1: 4 (over y), mode2: 4 (over x), mode3: 2 (over core).
Axes of the slice: x: 4, y: 4, z: 1, core: 2. Of those that a mesh axis runs over, the one named last changes fastest.
The devices are a block of a 4x4x8 slice.
Arguments:
- x_vol: bfloat16 [2, 512, 256, 512], P('rhs', 'mode1', 'mode2', 'mode3')
- diag_vals: float32 [512, 256, 512], P('mode1', 'mode2', 'mode3')
- a_mode1: bfloat16 [512, 512], replicated
- a_mode2: bfloat16 [256, 256], replicated
- a_mode3: bfloat16 [512, 512], replicated
- b_mode1: bfloat16 [512, 512], replicated
- b_mode2: bfloat16 [256, 256], replicated
- b_mode3: bfloat16 [512, 512], replicated
Outputs:
- output: float32 [2, 512, 256, 512], P('rhs', 'mode1', 'mode2', 'mode3')
All inputs are finite; a program needn't handle non-finite values.
Results may differ from a plain program's by a relative error of at most 0.0109024.
Values are sent between devices in bfloat16 or wider.
A program may use at most 768 MiB of HBM per device.

v0:
```python
import jax
import jax.numpy as jnp
from jax import lax
from jax.sharding import PartitionSpec as P


def mode_sum(volume, mat_one, mat_two, mat_three):
    whole_one = lax.all_to_all(volume, 'mode1', 2, 1, tiled=True)
    part_one = jnp.einsum('ia,rajk->rijk', mat_one, whole_one, preferred_element_type=jnp.float32).astype(jnp.bfloat16)
    term_one = lax.all_to_all(part_one, 'mode1', 1, 2, tiled=True)
    whole_two = lax.all_to_all(volume, 'mode2', 1, 2, tiled=True)
    part_two = jnp.einsum('jb,ribk->rijk', mat_two, whole_two, preferred_element_type=jnp.float32).astype(jnp.bfloat16)
    term_two = lax.all_to_all(part_two, 'mode2', 2, 1, tiled=True)
    whole_three = lax.all_to_all(volume, 'mode3', 2, 3, tiled=True)
    part_three = jnp.einsum('rijc,kc->rijk', whole_three, mat_three, preferred_element_type=jnp.float32).astype(jnp.bfloat16)
    term_three = lax.all_to_all(part_three, 'mode3', 3, 2, tiled=True)
    return term_one.astype(jnp.float32) + term_two.astype(jnp.float32) + term_three.astype(jnp.float32)


def solution(mesh):
    vol_spec = P('rhs', 'mode1', 'mode2', 'mode3')
    diag_spec = P('mode1', 'mode2', 'mode3')

    def local_op(x_vol, diag_vals, a_mode1, a_mode2, a_mode3, b_mode1, b_mode2, b_mode3):
        u_vol = mode_sum(x_vol, a_mode1, a_mode2, a_mode3).astype(jnp.bfloat16)
        w_vol = (diag_vals * u_vol.astype(jnp.float32)).astype(jnp.bfloat16)
        return mode_sum(w_vol, b_mode1, b_mode2, b_mode3)

    return jax.shard_map(local_op, mesh=mesh, in_specs=(vol_spec, diag_spec, P(), P(), P(), P(), P(), P()), out_specs=vol_spec, check_vma=False)
```

profile of v0, /device:TPU:97, one launch (start us, length us, event | category | flops | bytes accessed | tf_op | source)
XLA Modules:
  0.0 1068.8 jit_solution(17039006079549884333)
XLA Ops:
  11.6 13.6 %all_to_all.162 = bf16[2,128,64,256]{3,1,0,2:T(8,128)(2,1)S(1)} all-to-all(bf16[2,128,64,256]{3,1,0,2:T(8,128)(2,1)} %copy.75), channel_id=1, replica_groups=mesh['rhs'=1,'mode1'=4,'mode2'=4,'mode3'=2] {'mode3'}, dimensions={2} | all-to-all | bytes 16777216 | tf_op jit(solution)/shard_map/all_to_all | solution.py:14
  32.9 14.1 %all_to_all.133 = bf16[2,128,32,512]{3,1,2,0:T(8,128)(2,1)} reshape(bf16[2,128,32,2,256]{4,3,1,2,0:T(2,128)(2,1)} %bitcast.123) | data formatting | bytes 16777216 | tf_op jit(solution)/shard_map/all_to_all | solution.py:14
  57.2 14.6 %copy.89 = bf16[2,128,32,512]{1,2,0,3:T(8,128)(2,1)} copy(bf16[2,128,32,512]{3,1,2,0:T(8,128)(2,1)} %convolution_convert_fusion.1) | data formatting | bytes 16777216 | tf_op jit(solution)/shard_map/convert_element_type | solution.py:15
  71.8 18.2 %all_to_all.163 = bf16[2,128,32,512]{1,2,0,3:T(8,128)(2,1)} all-to-all(bf16[2,128,32,512]{1,2,0,3:T(8,128)(2,1)} %copy.89), channel_id=1, replica_groups=mesh['rhs'=1,'mode1'=4,'mode2'=4,'mode3'=2] {'mode3'}, dimensions={3} | all-to-all | bytes 16777216 | tf_op jit(solution)/shard_map/all_to_all | solution.py:16
  104.2 85.7 %all-to-all-done = bf16[2,128,64,256]{3,1,0,2:T(8,128)(2,1)} async-done(((bf16[2,128,64,256]{3,1,0,2:T(8,128)(2,1)}), bf16[2,128,64,256]{3,1,0,2:T(8,128)(2,1)}, u32[]{:S(2)}, u32[]{:S(2)}) %all-to-all-start) | async-done | bytes 8388640 | tf_op jit(solution)/shard_map/all_to_all | solution.py:8
  233.1 14.6 %copy.77 = bf16[2,512,16,256]{3,2,0,1:T(8,128)(2,1)} copy(bf16[2,512,16,256]{1,3,2,0:T(8,128)(2,1)} %convert_bitcast_fusion.7) | data formatting | bytes 16777216 | tf_op jit(solution)/shard_map/convert_element_type | solution.py:9
  247.7 41.0 %all-to-all-done.2 = bf16[2,128,64,256]{3,2,0,1:T(8,128)(2,1)} async-done(((bf16[2,128,64,256]{3,2,0,1:T(8,128)(2,1)}), bf16[2,128,64,256]{3,2,0,1:T(8,128)(2,1)}, u32[]{:S(2)}, u32[]{:S(2)}) %all-to-all-start.2) | async-done | bytes 8388640 | tf_op jit(solution)/shard_map/all_to_all | solution.py:11
  311.9 14.6 %copy.84 = bf16[2,32,256,256]{3,1,0,2:T(8,128)(2,1)} copy(bf16[2,32,256,256]{2,3,1,0:T(8,128)(2,1)} %convert_bitcast_fusion.6) | data formatting | bytes 16777216 | tf_op jit(solution)/shard_map/convert_element_type | solution.py:12
  326.5 59.5 %all-to-all-done.1 = bf16[2,512,16,256]{3,2,0,1:T(8,128)(2,1)} async-done(((bf16[2,512,16,256]{3,2,0,1:T(8,128)(2,1)}), bf16[2,512,16,256]{3,2,0,1:T(8,128)(2,1)}, u32[]{:S(2)}, u32[]{:S(2)}) %all-to-all-start.1) | async-done | bytes 8388640 | tf_op jit(solution)/shard_map/all_to_all | solution.py:10
  415.7 19.9 %copy.91 = f32[2,128,2,32,256]{4,3,2,1,0:T(8,128)} copy(f32[2,128,2,32,256]{1,4,2,3,0:T(8,128)} %convert_bitcast_fusion.1) | data formatting | bytes 33554432 | tf_op jit(solution)/shard_map/convert_element_type | solution.py:17
  467.0 15.6 %all-to-all-done.3 = bf16[2,32,256,256]{3,1,0,2:T(8,128)(2,1)} async-done(((bf16[2,32,256,256]{3,1,0,2:T(8,128)(2,1)}), bf16[2,32,256,256]{3,1,0,2:T(8,128)(2,1)}, u32[]{:S(2)}, u32[]{:S(2)}) %all-to-all-start.3) | async-done | bytes 8388640 | tf_op jit(solution)/shard_map/all_to_all | solution.py:13
  517.6 21.1 %multiply_convert_fusion = bf16[2,128,64,256]{3,2,1,0:T(8,128)(2,1)} fusion(f32[2,128,2,32,256]{4,3,2,1,0:T(8,128)} %copy.91, f32[2,128,64,256]{3,2,1,0:T(8,128)} %bitcast.116, f32[2,128,4,16,256]{4,3,2,1,0:T(8,128)} %copy.79, f32[128,64,256]{2,1,0:T(8,128)S(1)} %bitcast.130), kind=kLoop, calls=%fused_computation.9 | loop fusion | flops 25165824 | bytes 67108864 | tf_op jit(solution)/shard_map/convert_element_type | solution.py:26
  550.2 15.6 %all_to_all.164 = bf16[2,128,64,256]{3,1,0,2:T(8,128)(2,1)S(1)} all-to-all(bf16[2,128,64,256]{3,1,0,2:T(8,128)(2,1)} %copy.92), channel_id=1, replica_groups=mesh['rhs'=1,'mode1'=4,'mode2'=4,'mode3'=2] {'mode3'}, dimensions={2} | all-to-all | bytes 16777216 | tf_op jit(solution)/shard_map/all_to_all | solution.py:14
  573.5 14.2 %all_to_all.148 = bf16[2,128,32,512]{3,1,2,0:T(8,128)(2,1)} reshape(bf16[2,128,32,2,256]{4,3,1,2,0:T(2,128)(2,1)} %copy.106) | data formatting | bytes 16777216 | tf_op jit(solution)/shard_map/all_to_all | solution.py:14
  598.0 14.6 %copy.107 = bf16[2,128,32,512]{1,2,0,3:T(8,128)(2,1)} copy(bf16[2,128,32,512]{3,1,2,0:T(8,128)(2,1)} %convolution_convert_fusion) | data formatting | bytes 16777216 | tf_op jit(solution)/shard_map/convert_element_type | solution.py:15
  612.6 18.2 %all_to_all.165 = bf16[2,128,32,512]{1,2,0,3:T(8,128)(2,1)} all-to-all(bf16[2,128,32,512]{1,2,0,3:T(8,128)(2,1)} %copy.107), channel_id=1, replica_groups=mesh['rhs'=1,'mode1'=4,'mode2'=4,'mode3'=2] {'mode3'}, dimensions={3} | all-to-all | bytes 16777216 | tf_op jit(solution)/shard_map/all_to_all | solution.py:16
  644.7 85.0 %all-to-all-done.6 = bf16[2,128,64,256]{3,1,0,2:T(8,128)(2,1)} async-done(((bf16[2,128,64,256]{3,1,0,2:T(8,128)(2,1)}), bf16[2,128,64,256]{3,1,0,2:T(8,128)(2,1)}, u32[]{:S(2)}, u32[]{:S(2)}) %all-to-all-start.6) | async-done | bytes 8388640 | tf_op jit(solution)/shard_map/all_to_all | solution.py:8
  773.0 14.7 %copy.95 = bf16[2,512,16,256]{3,2,0,1:T(8,128)(2,1)} copy(bf16[2,512,16,256]{1,3,2,0:T(8,128)(2,1)} %convert_bitcast_fusion.5) | data formatting | bytes 16777216 | tf_op jit(solution)/shard_map/convert_element_type | solution.py:9
  787.7 40.7 %all-to-all-done.8 = bf16[2,128,64,256]{3,2,0,1:T(8,128)(2,1)} async-done(((bf16[2,128,64,256]{3,2,0,1:T(8,128)(2,1)}), bf16[2,128,64,256]{3,2,0,1:T(8,128)(2,1)}, u32[]{:S(2)}, u32[]{:S(2)}) %all-to-all-start.8) | async-done | bytes 8388640 | tf_op jit(solution)/shard_map/all_to_all | solution.py:11
  851.6 14.5 %copy.101 = bf16[2,32,256,256]{3,1,0,2:T(8,128)(2,1)} copy(bf16[2,32,256,256]{2,3,1,0:T(8,128)(2,1)} %convert_bitcast_fusion.4) | data formatting | bytes 16777216 | tf_op jit(solution)/shard_map/convert_element_type | solution.py:12
  866.1 59.4 %all-to-all-done.7 = bf16[2,512,16,256]{3,2,0,1:T(8,128)(2,1)} async-done(((bf16[2,512,16,256]{3,2,0,1:T(8,128)(2,1)}), bf16[2,512,16,256]{3,2,0,1:T(8,128)(2,1)}, u32[]{:S(2)}, u32[]{:S(2)}) %all-to-all-start.7) | async-done | bytes 8388640 | tf_op jit(solution)/shard_map/all_to_all | solution.py:10
  931.4 17.1 %copy.108 = f32[2,128,32,2,256]{4,2,3,1,0:T(8,128)} copy(bf16[2,128,32,2,256]{1,2,0,4,3:T(8,128)(2,1)} %bitcast.118) | data formatting | bytes 25165824 | tf_op jit(solution)/shard_map/convert_element_type | solution.py:17
  960.0 61.8 %all-to-all-done.9 = bf16[2,32,256,256]{3,1,0,2:T(8,128)(2,1)} async-done(((bf16[2,32,256,256]{3,1,0,2:T(8,128)(2,1)}), bf16[2,32,256,256]{3,1,0,2:T(8,128)(2,1)}, u32[]{:S(2)}, u32[]{:S(2)}) %all-to-all-start.9) | async-done | bytes 8388640 | tf_op jit(solution)/shard_map/all_to_all | solution.py:13
  1051.5 17.1 %bitcast_add_fusion = f32[2,128,64,256]{3,2,1,0:T(8,128)} fusion(f32[2,128,32,2,256]{4,2,3,1,0:T(8,128)} %copy.108, f32[2,128,64,256]{3,2,1,0:T(8,128)S(1)} %bitcast.117, f32[2,4,128,16,256]{4,3,1,2,0:T(8,128)} %copy.96), kind=kLoop, calls=%fused_computation | loop fusion | flops 8388608 | bytes 67108864 | tf_op jit(solution)/shard_map/add | solution.py:17
  (57 shorter events, 363.1 us)
Async XLA Ops:
  0.0 47.0 %copy-start = (bf16[512,512]{1,0:T(8,128)(2,1)S(1)}, bf16[512,512]{1,0:T(8,128)(2,1)}, u32[]{:S(2)}) copy-start(bf16[512,512]{1,0:T(8,128)(2,1)} %param.12) | copy-start | bytes 1572868
  90.0 99.8 %all-to-all-start = ((bf16[2,128,64,256]{3,1,0,2:T(8,128)(2,1)}), bf16[2,128,64,256]{3,1,0,2:T(8,128)(2,1)}, u32[]{:S(2)}, u32[]{:S(2)}) async-start(bf16[2,128,64,256]{3,1,0,2:T(8,128)(2,1)} %copy.75), calls=%async_computation | async-start | bytes 16777216 | tf_op jit(solution)/shard_map/all_to_all | solution.py:8
  189.9 98.8 %all-to-all-start.2 = ((bf16[2,128,64,256]{3,2,0,1:T(8,128)(2,1)}), bf16[2,128,64,256]{3,2,0,1:T(8,128)(2,1)}, u32[]{:S(2)}, u32[]{:S(2)}) async-start(bf16[2,128,64,256]{3,2,0,1:T(8,128)(2,1)} %copy.80), calls=%async_computation.2 | async-start | bytes 16777216 | tf_op jit(solution)/shard_map/all_to_all | solution.py:11
  209.7 13.2 %copy-start.4 = (bf16[512,512]{1,0:T(8,128)(2,1)S(1)}, bf16[512,512]{1,0:T(8,128)(2,1)}, u32[]{:S(2)}) copy-start(bf16[512,512]{1,0:T(8,128)(2,1)} %param.10) | copy-start | bytes 1572868
  288.7 97.3 %all-to-all-start.1 = ((bf16[2,512,16,256]{3,2,0,1:T(8,128)(2,1)}), bf16[2,512,16,256]{3,2,0,1:T(8,128)(2,1)}, u32[]{:S(2)}, u32[]{:S(2)}) async-start(bf16[2,512,16,256]{3,2,0,1:T(8,128)(2,1)} %copy.77), calls=%async_computation.1 | async-start | bytes 16777216 | tf_op jit(solution)/shard_map/all_to_all | solution.py:10
  294.4 8.5 copy-start.2
  386.0 96.5 %all-to-all-start.3 = ((bf16[2,32,256,256]{3,1,0,2:T(8,128)(2,1)}), bf16[2,32,256,256]{3,1,0,2:T(8,128)(2,1)}, u32[]{:S(2)}, u32[]{:S(2)}) async-start(bf16[2,32,256,256]{3,1,0,2:T(8,128)(2,1)} %copy.84), calls=%async_computation.3 | async-start | bytes 16777216 | tf_op jit(solution)/shard_map/all_to_all | solution.py:13
  493.9 23.7 %slice-start = ((s8[8388608]{0:T(1024)(128)(4,1)}), s8[4194304]{0:T(1024)(128)(4,1)S(1)}, s32[]{:S(2)}) async-start(s8[8388608]{0:T(1024)(128)(4,1)} %bitcast.129), calls=%async_computation.12 | async-start | bytes 8388608
  505.8 11.8 %slice-start.1 = ((s8[8388608]{0:T(1024)(128)(4,1)}), s8[4194304]{0:T(1024)(128)(4,1)S(1)}, s32[]{:S(2)}) async-start(s8[8388608]{0:T(1024)(128)(4,1)} %bitcast.129), calls=%async_computation.13 | async-start | bytes 8388608
  573.5 14.2 %copy-start.5 = (bf16[512,512]{1,0:T(8,128)(2,1)S(1)}, bf16[512,512]{1,0:T(8,128)(2,1)}, u32[]{:S(2)}) copy-start(bf16[512,512]{1,0:T(8,128)(2,1)} %param.15) | copy-start | bytes 1572868
  630.8 99.0 %all-to-all-start.6 = ((bf16[2,128,64,256]{3,1,0,2:T(8,128)(2,1)}), bf16[2,128,64,256]{3,1,0,2:T(8,128)(2,1)}, u32[]{:S(2)}, u32[]{:S(2)}) async-start(bf16[2,128,64,256]{3,1,0,2:T(8,128)(2,1)} %copy.92), calls=%async_computation.6 | async-start | bytes 16777216 | tf_op jit(solution)/shard_map/all_to_all | solution.py:8
  729.8 98.6 %all-to-all-start.8 = ((bf16[2,128,64,256]{3,2,0,1:T(8,128)(2,1)}), bf16[2,128,64,256]{3,2,0,1:T(8,128)(2,1)}, u32[]{:S(2)}, u32[]{:S(2)}) async-start(bf16[2,128,64,256]{3,2,0,1:T(8,128)(2,1)} %copy.97), calls=%async_computation.8 | async-start | bytes 16777216 | tf_op jit(solution)/shard_map/all_to_all | solution.py:11
  749.6 13.2 %copy-start.6 = (bf16[512,512]{1,0:T(8,128)(2,1)S(1)}, bf16[512,512]{1,0:T(8,128)(2,1)}, u32[]{:S(2)}) copy-start(bf16[512,512]{1,0:T(8,128)(2,1)} %param.13) | copy-start | bytes 1572868
  828.4 97.1 %all-to-all-start.7 = ((bf16[2,512,16,256]{3,2,0,1:T(8,128)(2,1)}), bf16[2,512,16,256]{3,2,0,1:T(8,128)(2,1)}, u32[]{:S(2)}, u32[]{:S(2)}) async-start(bf16[2,512,16,256]{3,2,0,1:T(8,128)(2,1)} %copy.95), calls=%async_computation.7 | async-start | bytes 16777216 | tf_op jit(solution)/shard_map/all_to_all | solution.py:10
  834.1 8.5 copy-start.3
  925.4 96.3 %all-to-all-start.9 = ((bf16[2,32,256,256]{3,1,0,2:T(8,128)(2,1)}), bf16[2,32,256,256]{3,1,0,2:T(8,128)(2,1)}, u32[]{:S(2)}, u32[]{:S(2)}) async-start(bf16[2,32,256,256]{3,1,0,2:T(8,128)(2,1)} %copy.101), calls=%async_computation.9 | async-start | bytes 16777216 | tf_op jit(solution)/shard_map/all_to_all | solution.py:13
  1051.5 17.1 %copy-start.1 = (bf16[512,512]{1,0:T(8,128)(2,1)S(1)}, bf16[512,512]{1,0:T(8,128)(2,1)}, u32[]{:S(2)}) copy-start(bf16[512,512]{1,0:T(8,128)(2,1)} %param.12) | copy-start | bytes 1572868
where the time goes:
time: 1080 us; the launch traced here: 1070 us
  waiting for transfers between devices  449 us (42%)
  local copies, waits for them, and re-layouts  363 us (34%)
  other arithmetic  85.5 us (8%)
  blocking collectives  65.6 us (6%)
  matrix products  58.8 us (5%)
  starting transfers between devices  47.2 us (4%)
    all_to_all x2, waiting for transfers between devices, mode_sum(): whole_one = lax.all_to_all(volume, 'mode1', 2, 1, tiled=True)  171 us
    all_to_all x2, waiting for transfers between devices, mode_sum(): term_one = lax.all_to_all(part_one, 'mode1', 1, 2, tiled=True)  119 us
    all_to_all x2, waiting for transfers between devices, mode_sum(): whole_two = lax.all_to_all(volume, 'mode2', 1, 2, tiled=True)  81.7 us
    all_to_all x2, waiting for transfers between devices, mode_sum(): term_two = lax.all_to_all(part_two, 'mode2', 2, 1, tiled=True)  77.3 us
    all_to_all x4, local copies, waits for them, and re-layouts, mode_sum(): whole_one = lax.all_to_all(volume, 'mode1', 2, 1, tiled=True)  53.6 us
    all_to_all x4, local copies, waits for them, and re-layouts, mode_sum(): whole_three = lax.all_to_all(volume, 'mode3', 2, 3, tiled=True)  43.8 us
    convert_element_type x2, local copies, waits for them, and re-layouts, mode_sum(): term_three.astype(jnp.float32)  37 us
    all_to_all x2, blocking collectives, mode_sum(): term_three = lax.all_to_all(part_three, 'mode3', 3, 2, tiled=True)  36.4 us
  transfers between devices with their start and end apart: 8, of which 8 were waited for; matrix products, arithmetic and copies ran while one was open for 24% of the time, Pallas kernels for 0%

commit v1 on v0

v1 whole, which is shorter than its diff:
```python
import functools

import jax
import jax.numpy as jnp
from jax import lax
from jax.experimental import pallas as pl
from jax.experimental.pallas import tpu as pltpu
from jax.sharding import PartitionSpec as P

MESH = pl.DeviceIdType.MESH
F32, BF16 = jnp.float32, jnp.bfloat16
LANES = 128


def aligned(index, size):
    return pl.ds(pl.multiple_of(index * size, size), size)


def kernel(dims, x_ref, d_ref, a1_ref, a2_ref, a3_ref, b1_ref, b2_ref, b3_ref,
           z_ref, lin1, lin2, lin3, out1, out2, t1, t2, w,
           vin1, vscr, vout1, vin2, vout2, v1, v2, vown, vpar, vd, vw, vz,
           y_send, y_recv, x_send, x_recv, c_send, c_recv,
           y_send2, y_recv2, x_send2, x_recv2, load_sem, store_sem):
    n1, n2, n3, rhs, ni, nj, nk = dims
    halves = nk // LANES
    chunks = rhs * halves
    jc, ic = nj // n1, ni // n2
    me1, me2, me3 = lax.axis_index('mode1'), lax.axis_index('mode2'), lax.axis_index('mode3')
    peer1 = [lax.rem(me1 + s, n1) for s in range(1, n1)]
    peer2 = [lax.rem(me2 + s, n2) for s in range(1, n2)]
    peer3 = lax.rem(me3 + 1, n3)

    barrier = pltpu.get_barrier_semaphore()
    for axis, peers in (('mode1', peer1), ('mode2', peer2), ('mode3', [peer3])):
        for peer in peers:
            pl.semaphore_signal(barrier, inc=1, device_id={axis: peer}, device_id_type=MESH)
    pl.semaphore_wait(barrier, n1 + n2 + n3 - 3)

    def remote(src, dst, send, recv, axis, peer):
        return pltpu.make_async_remote_copy(src_ref=src, dst_ref=dst, send_sem=send, recv_sem=recv,
                                            device_id={axis: peer}, device_id_type=MESH)

    def field(stage, c):
        if stage == 0:
            return x_ref.at[c // halves, :, :, aligned(lax.rem(c, halves), LANES)]
        return w.at[c]

    def out_y(stage, c, n):
        g = stage * chunks + c
        return remote(field(stage, c).at[:, aligned(peer1[n], jc), :], lin1.at[g, aligned(me1, ni)],
                      y_send.at[g, n], y_recv.at[g, n], 'mode1', peer1[n])

    def out_x(stage, c, n):
        g = stage * chunks + c
        return remote(field(stage, c).at[aligned(peer2[n], ic)], lin2.at[g, :, aligned(me2, nj), :],
                      x_send.at[g, n], x_recv.at[g, n], 'mode2', peer2[n])

    def out_c(stage, c):
        g = stage * chunks + c
        return remote(field(stage, c), lin3.at[g], c_send.at[g], c_recv.at[g], 'mode3', peer3)

    def back_y(stage, c, n):
        g = stage * chunks + c
        return remote(out1.at[g, aligned(peer1[n], ni)], t1.at[g, :, aligned(me1, jc), :],
                      y_send2.at[g, n], y_recv2.at[g, n], 'mode1', peer1[n])

    def back_x(stage, c, n):
        g = stage * chunks + c
        return remote(out2.at[g, :, aligned(peer2[n], nj), :], t2.at[g, aligned(me2, ic)],
                      x_send2.at[g, n], x_recv2.at[g, n], 'mode2', peer2[n])

    order1 = sorted(range(n1 - 1), key=lambda n: min(n + 1, n1 - n - 1))
    order2 = sorted(range(n2 - 1), key=lambda n: min(n + 1, n2 - n - 1))

    def start_out(stage, c):
        for n in order1:
            out_y(stage, c, n).start()
        for n in order2:
            out_x(stage, c, n).start()
        out_c(stage, c).start()

    def product_one(stage, c):
        g = stage * chunks + c
        mat = (a1_ref, b1_ref)[stage]
        for n in range(n1 - 1):
            out_y(stage, c, n).wait_recv()
        loads = [pltpu.make_async_copy(field(stage, c).at[:, aligned(me1, jc), :], vin1.at[aligned(me1, ni)], load_sem.at[0])]
        loads += [pltpu.make_async_copy(lin1.at[g, aligned(peer1[n], ni)], vin1.at[aligned(peer1[n], ni)], load_sem.at[n + 1])
                  for n in range(n1 - 1)]
        for copy in loads:
            copy.start()
        for copy in loads:
            copy.wait()
        full = n1 * ni
        part = 32

        @pl.loop(0, full // part)
        def _(b):
            vscr[pl.ds(pl.multiple_of(b * part * jc, part * jc), part * jc), :] = (
                vin1[pl.ds(b * part, part)].astype(F32).reshape(part * jc, LANES))

        @pl.loop(0, jc // 2)
        def _(b):
            rows = [pl.ds(2 * b + h, full, stride=jc) for h in range(2)]
            rhs_mat = jnp.concatenate([vscr[row, :].astype(BF16) for row in rows], axis=1)
            res = jnp.dot(mat[...], rhs_mat, preferred_element_type=F32)
            for h in range(2):
                vscr[rows[h], :] = res[:, h * LANES:(h + 1) * LANES]

        @pl.loop(0, full // part)
        def _(b):
            vout1[pl.ds(b * part, part)] = (
                vscr[pl.ds(pl.multiple_of(b * part * jc, part * jc), part * jc), :].reshape(part, jc, LANES).astype(BF16))

        stores = [pltpu.make_async_copy(vout1.at[aligned(peer1[n], ni)], out1.at[g, aligned(peer1[n], ni)], store_sem.at[n + 1])
                  for n in range(n1 - 1)]
        stores += [pltpu.make_async_copy(vout1.at[aligned(me1, ni)], t1.at[g, :, aligned(me1, jc), :], store_sem.at[0])]
        for copy in stores:
            copy.start()
        for copy in stores:
            copy.wait()
        for n in order1:
            back_y(stage, c, n).start()

    def product_two(stage, c):
        g = stage * chunks + c
        mat = (a2_ref, b2_ref)[stage]
        for n in range(n2 - 1):
            out_x(stage, c, n).wait_recv()
        loads = [pltpu.make_async_copy(field(stage, c).at[aligned(me2, ic)], vin2.at[:, aligned(me2, nj), :], load_sem.at[0])]
        loads += [pltpu.make_async_copy(lin2.at[g, :, aligned(peer2[n], nj), :], vin2.at[:, aligned(peer2[n], nj), :], load_sem.at[n + 1])
                  for n in range(n2 - 1)]
        for copy in loads:
            copy.start()
        for copy in loads:
            copy.wait()

        @pl.loop(0, ic // 2)
        def _(b):
            rhs_mat = jnp.concatenate([vin2[2 * b], vin2[2 * b + 1]], axis=1)
            res = jnp.dot(mat[...], rhs_mat, preferred_element_type=F32).astype(BF16)
            vout2[2 * b] = res[:, :LANES]
            vout2[2 * b + 1] = res[:, LANES:]

        stores = [pltpu.make_async_copy(vout2.at[:, aligned(peer2[n], nj), :], out2.at[g, :, aligned(peer2[n], nj), :], store_sem.at[n + 1])
                  for n in range(n2 - 1)]
        stores += [pltpu.make_async_copy(vout2.at[:, aligned(me2, nj), :], t2.at[g, aligned(me2, ic)], store_sem.at[0])]
        for copy in stores:
            copy.start()
        for copy in stores:
            copy.wait()
        for n in order2:
            back_x(stage, c, n).start()

    def total(stage, c):
        g = stage * chunks + c
        r, half = c // halves, lax.rem(c, halves)
        mat = (a3_ref, b3_ref)[stage]
        for n in range(n1 - 1):
            back_y(stage, c, n).wait_recv()
        for n in range(n2 - 1):
            back_x(stage, c, n).wait_recv()
        loads = [pltpu.make_async_copy(t1.at[g], v1, load_sem.at[0]),
                 pltpu.make_async_copy(t2.at[g], v2, load_sem.at[1])]
        for h in range(halves):
            lanes = pl.ds(h * LANES, LANES)
            loads += [pltpu.make_async_copy(field(stage, r * halves + h), vown.at[:, :, lanes], load_sem.at[2 + h]),
                      pltpu.make_async_copy(lin3.at[stage * chunks + r * halves + h], vpar.at[:, :, lanes], load_sem.at[2 + halves + h])]
        if stage == 0:
            loads += [pltpu.make_async_copy(d_ref.at[:, :, aligned(half, LANES)], vd, load_sem.at[2 + 2 * halves])]
        for copy in loads:
            copy.start()
        for copy in loads:
            copy.wait()
        rows = pl.ds(pl.multiple_of(me3 * nk + half * LANES, LANES), LANES)
        mat_own = mat[rows, aligned(me3, nk)]
        mat_par = mat[rows, aligned(peer3, nk)]
        contract = (((1,), (1,)), ((), ()))
        part = 8

        @pl.loop(0, ni // part)
        def _(b):
            sel = pl.ds(b * part, part)
            term = lax.dot_general(vown[sel].reshape(part * nj, nk), mat_own, contract, preferred_element_type=F32)
            term += lax.dot_general(vpar[sel].reshape(part * nj, nk), mat_par, contract, preferred_element_type=F32)
            term = term.astype(BF16).astype(F32).reshape(part, nj, LANES)
            acc = v1[sel].astype(F32) + v2[sel].astype(F32) + term
            if stage == 0:
                vw[sel] = (vd[sel] * acc.astype(BF16).astype(F32)).astype(BF16)
            else:
                vz[sel] = acc

        if stage == 0:
            store = pltpu.make_async_copy(vw, w.at[c], store_sem.at[0])
        else:
            store = pltpu.make_async_copy(vz, z_ref.at[r, :, :, aligned(half, LANES)], store_sem.at[0])
        store.start()
        store.wait()

    for stage in range(2):
        if stage == 0:
            @pl.loop(0, chunks)
            def _(c):
                start_out(0, c)

        @pl.loop(0, chunks)
        def _(c):
            product_one(stage, c)
            product_two(stage, c)

        @pl.loop(0, chunks)
        def _(c):
            out_c(stage, c).wait_recv()

        @pl.loop(0, chunks)
        def _(c):
            total(stage, c)
            if stage == 0:
                start_out(1, c)

    for stage in range(2):
        @pl.loop(0, chunks)
        def _(c):
            for n in range(n1 - 1):
                out_y(stage, c, n).wait_send()
                back_y(stage, c, n).wait_send()
            for n in range(n2 - 1):
                out_x(stage, c, n).wait_send()
                back_x(stage, c, n).wait_send()
            out_c(stage, c).wait_send()


def solution(mesh):
    n1, n2, n3 = mesh.shape['mode1'], mesh.shape['mode2'], mesh.shape['mode3']
    vol_spec = P('rhs', 'mode1', 'mode2', 'mode3')
    diag_spec = P('mode1', 'mode2', 'mode3')

    def local_op(x_vol, diag_vals, *mats):
        rhs, ni, nj, nk = x_vol.shape
        dims = (n1, n2, n3, rhs, ni, nj, nk)
        halves = nk // LANES
        chunks = rhs * halves
        steps = 2 * chunks
        jc, ic = nj // n1, ni // n2
        hbm = pl.BlockSpec(memory_space=pltpu.HBM)
        vmem = pl.BlockSpec(memory_space=pltpu.VMEM)
        dma = pltpu.SemaphoreType.DMA
        block = (ni, nj, LANES)
        outs = [
            jax.ShapeDtypeStruct(x_vol.shape, F32),
            jax.ShapeDtypeStruct((steps, n1 * ni, jc, LANES), BF16),
            jax.ShapeDtypeStruct((steps, ic, n2 * nj, LANES), BF16),
            jax.ShapeDtypeStruct((steps,) + block, BF16),
            jax.ShapeDtypeStruct((steps, n1 * ni, jc, LANES), BF16),
            jax.ShapeDtypeStruct((steps, ic, n2 * nj, LANES), BF16),
            jax.ShapeDtypeStruct((steps,) + block, BF16),
            jax.ShapeDtypeStruct((steps,) + block, BF16),
            jax.ShapeDtypeStruct((chunks,) + block, BF16),
        ]
        scratch = [
            pltpu.VMEM((n1 * ni, jc, LANES), BF16),
            pltpu.VMEM((n1 * ni * jc, LANES), F32),
            pltpu.VMEM((n1 * ni, jc, LANES), BF16),
            pltpu.VMEM((ic, n2 * nj, LANES), BF16),
            pltpu.VMEM((ic, n2 * nj, LANES), BF16),
            pltpu.VMEM(block, BF16),
            pltpu.VMEM(block, BF16),
            pltpu.VMEM((ni, nj, nk), BF16),
            pltpu.VMEM((ni, nj, nk), BF16),
            pltpu.VMEM(block, F32),
            pltpu.VMEM(block, BF16),
            pltpu.VMEM(block, F32),
            dma((steps, n1 - 1)), dma((steps, n1 - 1)),
            dma((steps, n2 - 1)), dma((steps, n2 - 1)),
            dma((steps,)), dma((steps,)),
            dma((steps, n1 - 1)), dma((steps, n1 - 1)),
            dma((steps, n2 - 1)), dma((steps, n2 - 1)),
            dma((3 + 2 * halves,)), dma((max(n1, n2),)),
        ]
        return pl.pallas_call(
            functools.partial(kernel, dims),
            out_shape=outs,
            in_specs=[hbm, hbm] + [vmem] * 6,
            out_specs=[hbm] * len(outs),
            scratch_shapes=scratch,
            compiler_params=pltpu.CompilerParams(collective_id=0, has_side_effects=True, vmem_limit_bytes=56 * 2 ** 20),
        )(x_vol, diag_vals, *mats)[0]

    return jax.shard_map(local_op, mesh=mesh, in_specs=(vol_spec, diag_spec, P(), P(), P(), P(), P(), P()), out_specs=vol_spec, check_vma=False)
```

time: 1080 us -> 396 us (0.37); the launches traced: 1070 us -> 396 us
  waiting for transfers between devices: 449 us -> 0 us
  Pallas kernels: 0 us -> 384 us
  local copies, waits for them, and re-layouts: 363 us -> 11.8 us
  other arithmetic: 85.5 us -> 0 us
  blocking collectives: 65.6 us -> 0 us
  matrix products: 58.8 us -> 0 us
  starting transfers between devices: 47.2 us -> 0 us
    all_to_all x8 -> x0, waiting for transfers between devices: 449 us -> none  [the longest x2 171 us: mode_sum(): whole_one = lax.all_to_all(volume, 'mode1', 2, 1, tiled=True)]
    pallas_call x0 -> x1, Pallas kernels: none -> 384 us  [local_op(): pl.pallas_call(functools.partial(kernel, dims), out_shape=outs, in_specs=...]
    convert_element_type x14 -> x0, local copies, waits for them, and re-layouts: 186 us -> none  [the longest x2 37 us: mode_sum(): term_three.astype(jnp.float32)]
    all_to_all x14 -> x0, local copies, waits for them, and re-layouts: 156 us -> none  [the longest x4 53.6 us: mode_sum(): whole_one = lax.all_to_all(volume, 'mode1', 2, 1, tiled=True)]
    convert_element_type x5 -> x0, other arithmetic: 68.4 us -> none  [the longest x2 23.6 us: mode_sum(): term_two.astype(jnp.float32)]
    all_to_all x4 -> x0, blocking collectives: 65.6 us -> none  [the longest x2 36.4 us: mode_sum(): term_three = lax.all_to_all(part_three, 'mode3', 3, 2, tiled=True)]
    dot_general x6 -> x0, matrix products: 58.8 us -> none  [the longest x2 20.4 us: mode_sum(): jnp.einsum('rijc,kc->rijk', whole_three, mat_three, preferred_element_typ...]
    all_to_all x8 -> x0, starting transfers between devices: 47.2 us -> none  [the longest x2 12.5 us: mode_sum(): whole_two = lax.all_to_all(volume, 'mode2', 1, 2, tiled=True)]
  transfers between devices with their start and end apart: 8 -> 0, of which waited for: 8 -> 0; matrix products, arithmetic and copies ran while one was open for 24% -> 0% of each run, Pallas kernels for 0% -> 0%
where the time goes in v1:
time: 396 us
  Pallas kernels  384 us (97%)
  local copies, waits for them, and re-layouts  11.8 us (3%)
    pallas_call x1, Pallas kernels, local_op(): pl.pallas_call(functools.partial(kernel, dims), out_shape=outs, in_specs=...  384 us
    unnamed x1, local copies, waits for them, and re-layouts  11.8 us

profile of v1, /device:TPU:97, one launch (start us, length us, event | category | flops | bytes accessed | tf_op | source)
XLA Modules:
  0.0 395.6 jit_solution(544428103057679884)
XLA Ops:
  0.0 383.8 %shard_map.82 = (f32[2,128,64,256]{3,2,1,0:T(8,128)}, bf16[8,512,16,128]{3,2,1,0:T(8,128)(2,1)}, bf16[8,32,256,128]{3,2,1,0:T(8,128)(2,1)}, bf16[8,128,64,128]{3...) custom-call(bf16[2,128,64,256]{3,2,1,0:T(8,128)(2,1)} %x_ref.1, ...), custom_call_target="tpu_custom_call" | custom-call | tf_op jit(solution)/shard_map/pallas_call | solution.py:280
  383.8 11.8 %copy.10 = f32[2,128,64,256]{3,2,1,0:T(8,128)} copy(f32[2,128,64,256]{3,2,1,0:T(8,128)} %get-tuple-element.6) | data formatting | bytes 33554432

commit v2 on v1

--- a/solution.py
+++ b/solution.py
@@ -18,9 +18,10 @@
 
 def kernel(dims, x_ref, d_ref, a1_ref, a2_ref, a3_ref, b1_ref, b2_ref, b3_ref,
            z_ref, lin1, lin2, lin3, out1, out2, t1, t2, w,
-           vin1, vscr, vout1, vin2, vout2, v1, v2, vown, vpar, vd, vw, vz,
+           ma1, ma2, ma3, mb1, mb2, mb3,
+           vin1, vscr, vout1, vin2, vout2, v1, v2, vown, vpar, vd, vw, last1, last2,
            y_send, y_recv, x_send, x_recv, c_send, c_recv,
-           y_send2, y_recv2, x_send2, x_recv2, load_sem, store_sem):
+           y_send2, y_recv2, x_send2, x_recv2, mat_sem, load_sem, store_sem):
     n1, n2, n3, rhs, ni, nj, nk = dims
     halves = nk // LANES
     chunks = rhs * halves
@@ -59,14 +60,19 @@
         g = stage * chunks + c
         return remote(field(stage, c), lin3.at[g], c_send.at[g], c_recv.at[g], 'mode3', peer3)
 
+    def is_last(stage, c):
+        return stage == 1 and isinstance(c, int) and c == chunks - 1
+
     def back_y(stage, c, n):
         g = stage * chunks + c
-        return remote(out1.at[g, aligned(peer1[n], ni)], t1.at[g, :, aligned(me1, jc), :],
+        dst = last1 if is_last(stage, c) else t1.at[g]
+        return remote(out1.at[g, aligned(peer1[n], ni)], dst.at[:, aligned(me1, jc), :],
                       y_send2.at[g, n], y_recv2.at[g, n], 'mode1', peer1[n])
 
     def back_x(stage, c, n):
         g = stage * chunks + c
-        return remote(out2.at[g, :, aligned(peer2[n], nj), :], t2.at[g, aligned(me2, ic)],
+        dst = last2 if is_last(stage, c) else t2.at[g]
+        return remote(out2.at[g, :, aligned(peer2[n], nj), :], dst.at[aligned(me2, ic)],
                       x_send2.at[g, n], x_recv2.at[g, n], 'mode2', peer2[n])
 
     order1 = sorted(range(n1 - 1), key=lambda n: min(n + 1, n1 - n - 1))
@@ -81,7 +87,7 @@
 
     def product_one(stage, c):
         g = stage * chunks + c
-        mat = (a1_ref, b1_ref)[stage]
+        mat = (ma1, mb1)[stage]
         for n in range(n1 - 1):
             out_y(stage, c, n).wait_recv()
         loads = [pltpu.make_async_copy(field(stage, c).at[:, aligned(me1, jc), :], vin1.at[aligned(me1, ni)], load_sem.at[0])]
@@ -114,7 +120,8 @@
 
         stores = [pltpu.make_async_copy(vout1.at[aligned(peer1[n], ni)], out1.at[g, aligned(peer1[n], ni)], store_sem.at[n + 1])
                   for n in range(n1 - 1)]
-        stores += [pltpu.make_async_copy(vout1.at[aligned(me1, ni)], t1.at[g, :, aligned(me1, jc), :], store_sem.at[0])]
+        if not is_last(stage, c):
+            stores += [pltpu.make_async_copy(vout1.at[aligned(me1, ni)], t1.at[g, :, aligned(me1, jc), :], store_sem.at[0])]
         for copy in stores:
             copy.start()
         for copy in stores:
@@ -124,7 +131,7 @@
 
     def product_two(stage, c):
         g = stage * chunks + c
-        mat = (a2_ref, b2_ref)[stage]
+        mat = (ma2, mb2)[stage]
         for n in range(n2 - 1):
             out_x(stage, c, n).wait_recv()
         loads = [pltpu.make_async_copy(field(stage, c).at[aligned(me2, ic)], vin2.at[:, aligned(me2, nj), :], load_sem.at[0])]
@@ -144,7 +151,8 @@
 
         stores = [pltpu.make_async_copy(vout2.at[:, aligned(peer2[n], nj), :], out2.at[g, :, aligned(peer2[n], nj), :], store_sem.at[n + 1])
                   for n in range(n2 - 1)]
-        stores += [pltpu.make_async_copy(vout2.at[:, aligned(me2, nj), :], t2.at[g, aligned(me2, ic)], store_sem.at[0])]
+        if not is_last(stage, c):
+            stores += [pltpu.make_async_copy(vout2.at[:, aligned(me2, nj), :], t2.at[g, aligned(me2, ic)], store_sem.at[0])]
         for copy in stores:
             copy.start()
         for copy in stores:
@@ -152,26 +160,15 @@
         for n in order2:
             back_x(stage, c, n).start()
 
-    def total(stage, c):
-        g = stage * chunks + c
-        r, half = c // halves, lax.rem(c, halves)
-        mat = (a3_ref, b3_ref)[stage]
+    def wait_back(stage, c):
         for n in range(n1 - 1):
             back_y(stage, c, n).wait_recv()
         for n in range(n2 - 1):
             back_x(stage, c, n).wait_recv()
-        loads = [pltpu.make_async_copy(t1.at[g], v1, load_sem.at[0]),
-                 pltpu.make_async_copy(t2.at[g], v2, load_sem.at[1])]
-        for h in range(halves):
-            lanes = pl.ds(h * LANES, LANES)
-            loads += [pltpu.make_async_copy(field(stage, r * halves + h), vown.at[:, :, lanes], load_sem.at[2 + h]),
-                      pltpu.make_async_copy(lin3.at[stage * chunks + r * halves + h], vpar.at[:, :, lanes], load_sem.at[2 + halves + h])]
-        if stage == 0:
-            loads += [pltpu.make_async_copy(d_ref.at[:, :, aligned(half, LANES)], vd, load_sem.at[2 + 2 * halves])]
-        for copy in loads:
-            copy.start()
-        for copy in loads:
-            copy.wait()
+
+    def third(stage, c, put):
+        r, half = c // halves, lax.rem(c, halves)
+        mat = (ma3, mb3)[stage]
         rows = pl.ds(pl.multiple_of(me3 * nk + half * LANES, LANES), LANES)
         mat_own = mat[rows, aligned(me3, nk)]
         mat_par = mat[rows, aligned(peer3, nk)]
@@ -183,40 +180,112 @@
             sel = pl.ds(b * part, part)
             term = lax.dot_general(vown[sel].reshape(part * nj, nk), mat_own, contract, preferred_element_type=F32)
             term += lax.dot_general(vpar[sel].reshape(part * nj, nk), mat_par, contract, preferred_element_type=F32)
-            term = term.astype(BF16).astype(F32).reshape(part, nj, LANES)
+            put(sel, term.astype(BF16).astype(F32).reshape(part, nj, LANES))
+
+    def run(copies):
+        for copy in copies:
+            copy.start()
+        for copy in copies:
+            copy.wait()
+
+    def load_field(stage, c):
+        r = c // halves
+        loads = []
+        for h in range(halves):
+            lanes = pl.ds(h * LANES, LANES)
+            loads += [pltpu.make_async_copy(field(stage, r * halves + h), vown.at[:, :, lanes], load_sem.at[2 + h]),
+                      pltpu.make_async_copy(lin3.at[stage * chunks + r * halves + h], vpar.at[:, :, lanes], load_sem.at[2 + halves + h])]
+        return loads
+
+    def load_terms(stage, c):
+        g = stage * chunks + c
+        return [pltpu.make_async_copy(t1.at[g], v1, load_sem.at[0]), pltpu.make_async_copy(t2.at[g], v2, load_sem.at[1])]
+
+    def total_a(c):
+        half = lax.rem(c, halves)
+        wait_back(0, c)
+        run(load_terms(0, c) + load_field(0, c)
+            + [pltpu.make_async_copy(d_ref.at[:, :, aligned(half, LANES)], vd, load_sem.at[2 + 2 * halves])])
+
+        def put(sel, term):
             acc = v1[sel].astype(F32) + v2[sel].astype(F32) + term
-            if stage == 0:
-                vw[sel] = (vd[sel] * acc.astype(BF16).astype(F32)).astype(BF16)
-            else:
-                vz[sel] = acc
-
-        if stage == 0:
-            store = pltpu.make_async_copy(vw, w.at[c], store_sem.at[0])
-        else:
-            store = pltpu.make_async_copy(vz, z_ref.at[r, :, :, aligned(half, LANES)], store_sem.at[0])
-        store.start()
-        store.wait()
-
-    for stage in range(2):
-        if stage == 0:
-            @pl.loop(0, chunks)
-            def _(c):
-                start_out(0, c)
-
-        @pl.loop(0, chunks)
-        def _(c):
-            product_one(stage, c)
-            product_two(stage, c)
-
-        @pl.loop(0, chunks)
-        def _(c):
-            out_c(stage, c).wait_recv()
-
-        @pl.loop(0, chunks)
-        def _(c):
-            total(stage, c)
-            if stage == 0:
-                start_out(1, c)
+            vw[sel] = (vd[sel] * acc.astype(BF16).astype(F32)).astype(BF16)
+
+        third(0, c, put)
+        run([pltpu.make_async_copy(vw, w.at[c], store_sem.at[0])])
+
+    def total_b(c):
+        r, lanes = c // halves, aligned(lax.rem(c, halves), LANES)
+        run(load_field(1, c))
+
+        def put(sel, term):
+            z_ref[r, sel, :, lanes] = term
+
+        third(1, c, put)
+
+        def add(block, rows, cols, part):
+            start, count = rows
+
+            @pl.loop(0, count // part)
+            def _(b):
+                sel = pl.ds(start + b * part, part)
+                z_ref[r, sel, cols, lanes] = block(b * part, part) + z_ref[r, sel, cols, lanes]
+
+        if not is_last(1, c):
+            wait_back(1, c)
+            run(load_terms(1, c))
+            add(lambda i, p: v1[pl.ds(i, p)].astype(F32) + v2[pl.ds(i, p)].astype(F32), (0, ni), slice(None), 8)
+            return
+        add(lambda i, p: vout1[pl.ds(me1 * ni + i, p)].astype(F32), (0, ni), aligned(me1, jc), 8)
+        add(lambda i, p: vout2[pl.ds(i, p), aligned(me2, nj), :].astype(F32), (me2 * ic, ic), slice(None), 8)
+        for m in range(max(n1, n2) - 1):
+            if m < n1 - 1:
+                peer = peer1[n1 - 2 - order1[m]]
+                back_y(1, c, order1[m]).wait_recv()
+                add(lambda i, p: last1[pl.ds(i, p), aligned(peer, jc), :].astype(F32), (0, ni), aligned(peer, jc), 8)
+            if m < n2 - 1:
+                peer = peer2[n2 - 2 - order2[m]]
+                back_x(1, c, order2[m]).wait_recv()
+                add(lambda i, p: last2[pl.ds(peer * ic + i, p)].astype(F32), (peer * ic, ic), slice(None), 8)
+
+    @pl.loop(0, chunks)
+    def _(c):
+        start_out(0, c)
+
+    run([pltpu.make_async_copy(src, dst, mat_sem.at[m]) for m, (src, dst) in enumerate(
+        zip((a1_ref, a2_ref, a3_ref, b1_ref, b2_ref, b3_ref), (ma1, ma2, ma3, mb1, mb2, mb3)))])
+
+    @pl.loop(0, chunks)
+    def _(c):
+        product_one(0, c)
+        product_two(0, c)
+
+    @pl.loop(0, chunks)
+    def _(c):
+        out_c(0, c).wait_recv()
+
+    @pl.loop(0, chunks)
+    def _(c):
+        total_a(c)
+        start_out(1, c)
+
+    @pl.loop(0, chunks - 1)
+    def _(c):
+        product_one(1, c)
+        product_two(1, c)
+
+    product_one(1, chunks - 1)
+    product_two(1, chunks - 1)
+
+    @pl.loop(0, chunks)
+    def _(c):
+        out_c(1, c).wait_recv()
+
+    @pl.loop(0, chunks - 1)
+    def _(c):
+        total_b(c)
+
+    total_b(chunks - 1)
 
     for stage in range(2):
         @pl.loop(0, chunks)
@@ -247,7 +316,7 @@
         dma = pltpu.SemaphoreType.DMA
         block = (ni, nj, LANES)
         outs = [
-            jax.ShapeDtypeStruct(x_vol.shape, F32),
+            pltpu.VMEM(x_vol.shape, F32),
             jax.ShapeDtypeStruct((steps, n1 * ni, jc, LANES), BF16),
             jax.ShapeDtypeStruct((steps, ic, n2 * nj, LANES), BF16),
             jax.ShapeDtypeStruct((steps,) + block, BF16),
@@ -257,7 +326,7 @@
             jax.ShapeDtypeStruct((steps,) + block, BF16),
             jax.ShapeDtypeStruct((chunks,) + block, BF16),
         ]
-        scratch = [
+        scratch = [pltpu.VMEM(mat.shape, mat.dtype) for mat in mats] + [
             pltpu.VMEM((n1 * ni, jc, LANES), BF16),
             pltpu.VMEM((n1 * ni * jc, LANES), F32),
             pltpu.VMEM((n1 * ni, jc, LANES), BF16),
@@ -269,21 +338,22 @@
             pltpu.VMEM((ni, nj, nk), BF16),
             pltpu.VMEM(block, F32),
             pltpu.VMEM(block, BF16),
-            pltpu.VMEM(block, F32),
+            pltpu.VMEM(block, BF16),
+            pltpu.VMEM(block, BF16),
             dma((steps, n1 - 1)), dma((steps, n1 - 1)),
             dma((steps, n2 - 1)), dma((steps, n2 - 1)),
             dma((steps,)), dma((steps,)),
             dma((steps, n1 - 1)), dma((steps, n1 - 1)),
             dma((steps, n2 - 1)), dma((steps, n2 - 1)),
-            dma((3 + 2 * halves,)), dma((max(n1, n2),)),
+            dma((len(mats),)), dma((max(3 + 2 * halves, n1, n2),)), dma((max(n1, n2),)),
         ]
         return pl.pallas_call(
             functools.partial(kernel, dims),
             out_shape=outs,
-            in_specs=[hbm, hbm] + [vmem] * 6,
-            out_specs=[hbm] * len(outs),
+            in_specs=[hbm] * (2 + len(mats)),
+            out_specs=[vmem] + [hbm] * (len(outs) - 1),
             scratch_shapes=scratch,
-            compiler_params=pltpu.CompilerParams(collective_id=0, has_side_effects=True, vmem_limit_bytes=56 * 2 ** 20),
+            compiler_params=pltpu.CompilerParams(collective_id=0, has_side_effects=True, vmem_limit_bytes=46 * 2 ** 20),
         )(x_vol, diag_vals, *mats)[0]
 
     return jax.shard_map(local_op, mesh=mesh, in_specs=(vol_spec, diag_spec, P(), P(), P(), P(), P(), P()), out_specs=vol_spec, check_vma=False)

time: 396 us -> 377 us (0.952)
  Pallas kernels: 384 us -> 371 us
  local copies, waits for them, and re-layouts: 11.8 us -> 6.16 us
    pallas_call x1, Pallas kernels: 384 us -> 371 us  [local_op(): pl.pallas_call(functools.partial(kernel, dims), out_shape=outs, in_specs=...]
    unnamed x1, local copies, waits for them, and re-layouts: 11.8 us -> 6.16 us
where the time goes in v2:
time: 377 us
  Pallas kernels  371 us (98%)
  local copies, waits for them, and re-layouts  6.16 us (2%)
    pallas_call x1, Pallas kernels, local_op(): pl.pallas_call(functools.partial(kernel, dims), out_shape=outs, in_specs=...  371 us

profile of v2, /device:TPU:97, one launch (start us, length us, event | category | flops | bytes accessed | tf_op | source)
XLA Modules:
  0.0 376.8 jit_solution(4739312617781356184)
XLA Ops:
  0.0 370.7 %shard_map.82 = (f32[2,128,64,256]{3,2,1,0:T(8,128)S(1)}, bf16[8,512,16,128]{3,2,1,0:T(8,128)(2,1)}, bf16[8,32,256,128]{3,2,1,0:T(8,128)(2,1)}, bf16[8,128,64,12...) custom-call(bf16[2,128,64,256]{3,2,1,0:T(8,128)(2,1)} %x_ref.1, ...), custom_call_target="tpu_custom_call" | custom-call | tf_op jit(solution)/shard_map/pallas_call | solution.py:350
  370.7 6.2 %copy.10 = f32[2,128,64,256]{3,2,1,0:T(8,128)} copy(f32[2,128,64,256]{3,2,1,0:T(8,128)S(1)} %get-tuple-element.6) | data formatting | bytes 33554432

commit v3 on v2

--- a/solution.py
+++ b/solution.py
@@ -214,6 +214,19 @@
         third(0, c, put)
         run([pltpu.make_async_copy(vw, w.at[c], store_sem.at[0])])
 
+    def wait_out_sends(stage, c):
+        for n in range(n1 - 1):
+            out_y(stage, c, n).wait_send()
+        for n in range(n2 - 1):
+            out_x(stage, c, n).wait_send()
+        out_c(stage, c).wait_send()
+
+    def wait_back_sends(stage, c):
+        for n in range(n1 - 1):
+            back_y(stage, c, n).wait_send()
+        for n in range(n2 - 1):
+            back_x(stage, c, n).wait_send()
+
     def total_b(c):
         r, lanes = c // halves, aligned(lax.rem(c, halves), LANES)
         run(load_field(1, c))
@@ -238,6 +251,16 @@
             return
         add(lambda i, p: vout1[pl.ds(me1 * ni + i, p)].astype(F32), (0, ni), aligned(me1, jc), 8)
         add(lambda i, p: vout2[pl.ds(i, p), aligned(me2, nj), :].astype(F32), (me2 * ic, ic), slice(None), 8)
+        @pl.loop(0, chunks)
+        def _(e):
+            wait_out_sends(0, e)
+            wait_back_sends(0, e)
+            wait_out_sends(1, e)
+
+        @pl.loop(0, chunks - 1)
+        def _(e):
+            wait_back_sends(1, e)
+
         for m in range(max(n1, n2) - 1):
             if m < n1 - 1:
                 peer = peer1[n1 - 2 - order1[m]]
@@ -286,17 +309,7 @@
         total_b(c)
 
     total_b(chunks - 1)
-
-    for stage in range(2):
-        @pl.loop(0, chunks)
-        def _(c):
-            for n in range(n1 - 1):
-                out_y(stage, c, n).wait_send()
-                back_y(stage, c, n).wait_send()
-            for n in range(n2 - 1):
-                out_x(stage, c, n).wait_send()
-                back_x(stage, c, n).wait_send()
-            out_c(stage, c).wait_send()
+    wait_back_sends(1, chunks - 1)
 
 
 def solution(mesh):
@@ -347,7 +360,7 @@
             dma((steps, n2 - 1)), dma((steps, n2 - 1)),
             dma((len(mats),)), dma((max(3 + 2 * halves, n1, n2),)), dma((max(n1, n2),)),
         ]
-        return pl.pallas_call(
+        res = pl.pallas_call(
             functools.partial(kernel, dims),
             out_shape=outs,
             in_specs=[hbm] * (2 + len(mats)),
@@ -355,5 +368,17 @@
             scratch_shapes=scratch,
             compiler_params=pltpu.CompilerParams(collective_id=0, has_side_effects=True, vmem_limit_bytes=46 * 2 ** 20),
         )(x_vol, diag_vals, *mats)[0]
+        parts = 8
+
+        def put(z_in, z_out, sem):
+            copies = [pltpu.make_async_copy(z_in.at[r, pl.ds(b * (ni // parts), ni // parts)], z_out.at[r, pl.ds(b * (ni // parts), ni // parts)], sem.at[r, b])
+                      for r in range(rhs) for b in range(parts)]
+            for copy in copies:
+                copy.start()
+            for copy in copies:
+                copy.wait()
+
+        return pl.pallas_call(put, out_shape=jax.ShapeDtypeStruct(x_vol.shape, F32), in_specs=[vmem], out_specs=hbm,
+                              scratch_shapes=[dma((rhs, parts))], compiler_params=pltpu.CompilerParams(vmem_limit_bytes=24 * 2 ** 20))(res)
 
     return jax.shard_map(local_op, mesh=mesh, in_specs=(vol_spec, diag_spec, P(), P(), P(), P(), P(), P()), out_specs=vol_spec, check_vma=False)

time: 377 us -> 377 us (level)
  local copies, waits for them, and re-layouts: 6.16 us -> 0 us
  Pallas kernels: 371 us -> 376 us
    unnamed x1 -> x0, local copies, waits for them, and re-layouts: 6.16 us -> none
    pallas_call x0 -> x1, Pallas kernels: none -> 5.96 us  [local_op(): pl.pallas_call(put, out_shape=jax.ShapeDtypeStruct(x_vol.shape, F32), in_...]
where the time goes in v3:
time: 377 us; the launch traced here: 376 us
  Pallas kernels  376 us (100%)
    pallas_call x1, Pallas kernels, local_op(): pl.pallas_call(functools.partial(kernel, dims), out_shape=outs, in_specs=...  371 us

profile of v3, /device:TPU:97, one launch (start us, length us, event | category | flops | bytes accessed | tf_op | source)
XLA Modules:
  0.0 376.5 jit_solution(15305821015828770266)
XLA Ops:
  0.0 370.5 %shard_map.82 = (f32[2,128,64,256]{3,2,1,0:T(8,128)S(1)}, bf16[8,512,16,128]{3,2,1,0:T(8,128)(2,1)}, bf16[8,32,256,128]{3,2,1,0:T(8,128)(2,1)}, bf16[8,128,64,12...) custom-call(bf16[2,128,64,256]{3,2,1,0:T(8,128)(2,1)} %x_ref.1, ...), custom_call_target="tpu_custom_call" | custom-call | tf_op jit(solution)/shard_map/pallas_call | solution.py:363
  370.5 6.0 %shard_map.83 = f32[2,128,64,256]{3,2,1,0:T(8,128)} custom-call(f32[2,128,64,256]{3,2,1,0:T(8,128)S(1)} %get-tuple-element.6.z_in), custom_call_target="tpu_custom_call" | custom-call | tf_op jit(solution)/shard_map/pallas_call | solution.py:381

commit v4 on v0

v4 whole, which is shorter than its diff:
```python
import functools

import jax
import jax.numpy as jnp
from jax import lax
from jax.experimental import pallas as pl
from jax.experimental.pallas import tpu as pltpu
from jax.sharding import PartitionSpec as P

MESH = pl.DeviceIdType.MESH
F32, BF16 = jnp.float32, jnp.bfloat16
LANES = 128


def aligned(index, size):
    return pl.ds(pl.multiple_of(index * size, size), size)


def kernel(dims, x_ref, d_ref, a1_ref, a2_ref, a3_ref, b1_ref, b2_ref, b3_ref,
           z_ref, lin1, lin2, lin3, out1, out2, t1, t2, w,
           ma1, ma2, ma3, mb1, mb2, mb3,
           vin1, vscr, vout1, vin2, vout2, v1, v2, vown, vpar, vd, vw, last1, last2,
           y_send, y_recv, x_send, x_recv, c_send, c_recv,
           y_send2, y_recv2, x_send2, x_recv2, mat_sem, load_sem, store_sem):
    n1, n2, n3, rhs, ni, nj, nk = dims
    halves = nk // LANES
    chunks = rhs * halves
    jc, ic = nj // n1, ni // n2
    me1, me2, me3 = lax.axis_index('mode1'), lax.axis_index('mode2'), lax.axis_index('mode3')
    peer1 = [lax.rem(me1 + s, n1) for s in range(1, n1)]
    peer2 = [lax.rem(me2 + s, n2) for s in range(1, n2)]
    peer3 = lax.rem(me3 + 1, n3)

    barrier = pltpu.get_barrier_semaphore()
    for axis, peers in (('mode1', peer1), ('mode2', peer2), ('mode3', [peer3])):
        for peer in peers:
            pl.semaphore_signal(barrier, inc=1, device_id={axis: peer}, device_id_type=MESH)
    pl.semaphore_wait(barrier, n1 + n2 + n3 - 3)

    order1 = sorted(range(n1 - 1), key=lambda n: min(n + 1, n1 - n - 1))
    order2 = sorted(range(n2 - 1), key=lambda n: min(n + 1, n2 - n - 1))

    def remote(src, dst, send, recv, axis, peer):
        return pltpu.make_async_remote_copy(src_ref=src, dst_ref=dst, send_sem=send, recv_sem=recv,
                                            device_id={axis: peer}, device_id_type=MESH)

    def run(copies):
        for copy in copies:
            copy.start()
        for copy in copies:
            copy.wait()

    def field(stage, r):
        return (x_ref, w)[stage].at[r]

    def out_y(stage, r, n):
        q = stage * rhs + r
        return remote(field(stage, r).at[:, aligned(peer1[n], jc), :], lin1.at[q, aligned(me1, ni)],
                      y_send.at[q, n], y_recv.at[q, n], 'mode1', peer1[n])

    def out_x(stage, r, n):
        q = stage * rhs + r
        return remote(field(stage, r).at[aligned(peer2[n], ic)], lin2.at[q, :, aligned(me2, nj), :],
                      x_send.at[q, n], x_recv.at[q, n], 'mode2', peer2[n])

    def out_c(stage, r):
        q = stage * rhs + r
        return remote(field(stage, r), lin3.at[q], c_send.at[q], c_recv.at[q], 'mode3', peer3)

    def is_last(stage, c):
        return stage == 1 and isinstance(c, int) and c == chunks - 1

    def back_y(stage, c, n):
        g = stage * chunks + c
        dst = last1 if is_last(stage, c) else t1.at[g]
        return remote(out1.at[g, aligned(peer1[n], ni)], dst.at[:, aligned(me1, jc), :],
                      y_send2.at[g, n], y_recv2.at[g, n], 'mode1', peer1[n])

    def back_x(stage, c, n):
        g = stage * chunks + c
        dst = last2 if is_last(stage, c) else t2.at[g]
        return remote(out2.at[g, :, aligned(peer2[n], nj), :], dst.at[aligned(me2, ic)],
                      x_send2.at[g, n], x_recv2.at[g, n], 'mode2', peer2[n])

    def start_out(stage, r):
        for n in order1:
            out_y(stage, r, n).start()
        for n in order2:
            out_x(stage, r, n).start()
        out_c(stage, r).start()

    def wait_out(stage, r):
        for n in range(n1 - 1):
            out_y(stage, r, n).wait_recv()
        for n in range(n2 - 1):
            out_x(stage, r, n).wait_recv()

    def wait_back(stage, c):
        for n in range(n1 - 1):
            back_y(stage, c, n).wait_recv()
        for n in range(n2 - 1):
            back_x(stage, c, n).wait_recv()

    def wait_out_sends(stage, r):
        for n in range(n1 - 1):
            out_y(stage, r, n).wait_send()
        for n in range(n2 - 1):
            out_x(stage, r, n).wait_send()
        out_c(stage, r).wait_send()

    def wait_back_sends(stage, c):
        for n in range(n1 - 1):
            back_y(stage, c, n).wait_send()
        for n in range(n2 - 1):
            back_x(stage, c, n).wait_send()

    def product_one(stage, r, h, c):
        q, g, lanes = stage * rhs + r, stage * chunks + c, aligned(h, LANES)
        mat = (ma1, mb1)[stage]
        run([pltpu.make_async_copy(field(stage, r).at[:, aligned(me1, jc), lanes], vin1.at[aligned(me1, ni)], load_sem.at[0])]
            + [pltpu.make_async_copy(lin1.at[q, aligned(peer1[n], ni), :, lanes], vin1.at[aligned(peer1[n], ni)], load_sem.at[n + 1])
               for n in range(n1 - 1)])
        full = n1 * ni
        part = 32

        @pl.loop(0, full // part)
        def _(b):
            vscr[aligned(b, part * jc), :] = vin1[pl.ds(b * part, part)].astype(F32).reshape(part * jc, LANES)

        @pl.loop(0, jc // 2)
        def _(b):
            rows = [pl.ds(2 * b + e, full, stride=jc) for e in range(2)]
            rhs_mat = jnp.concatenate([vscr[row, :].astype(BF16) for row in rows], axis=1)
            res = jnp.dot(mat[...], rhs_mat, preferred_element_type=F32)
            for e in range(2):
                vscr[rows[e], :] = res[:, e * LANES:(e + 1) * LANES]

        @pl.loop(0, full // part)
        def _(b):
            vout1[pl.ds(b * part, part)] = vscr[aligned(b, part * jc), :].reshape(part, jc, LANES).astype(BF16)

        stores = [pltpu.make_async_copy(vout1.at[aligned(peer1[n], ni)], out1.at[g, aligned(peer1[n], ni)], store_sem.at[n + 1])
                  for n in range(n1 - 1)]
        if not is_last(stage, c):
            stores += [pltpu.make_async_copy(vout1.at[aligned(me1, ni)], t1.at[g, :, aligned(me1, jc), :], store_sem.at[0])]
        run(stores)
        for n in order1:
            back_y(stage, c, n).start()

    def product_two(stage, r, h, c):
        q, g, lanes = stage * rhs + r, stage * chunks + c, aligned(h, LANES)
        mat = (ma2, mb2)[stage]
        run([pltpu.make_async_copy(field(stage, r).at[aligned(me2, ic), :, lanes], vin2.at[:, aligned(me2, nj), :], load_sem.at[0])]
            + [pltpu.make_async_copy(lin2.at[q, :, aligned(peer2[n], nj), lanes], vin2.at[:, aligned(peer2[n], nj), :], load_sem.at[n + 1])
               for n in range(n2 - 1)])

        @pl.loop(0, ic // 2)
        def _(b):
            rhs_mat = jnp.concatenate([vin2[2 * b], vin2[2 * b + 1]], axis=1)
            res = jnp.dot(mat[...], rhs_mat, preferred_element_type=F32).astype(BF16)
            vout2[2 * b] = res[:, :LANES]
            vout2[2 * b + 1] = res[:, LANES:]

        stores = [pltpu.make_async_copy(vout2.at[:, aligned(peer2[n], nj), :], out2.at[g, :, aligned(peer2[n], nj), :], store_sem.at[n + 1])
                  for n in range(n2 - 1)]
        if not is_last(stage, c):
            stores += [pltpu.make_async_copy(vout2.at[:, aligned(me2, nj), :], t2.at[g, aligned(me2, ic)], store_sem.at[0])]
        run(stores)
        for n in order2:
            back_x(stage, c, n).start()

    def products(stage, r, h):
        c = r * halves + h
        product_one(stage, r, h, c)
        product_two(stage, r, h, c)

    def third(stage, h, put):
        mat = (ma3, mb3)[stage]
        rows = pl.ds(pl.multiple_of(me3 * nk + h * LANES, LANES), LANES)
        mat_own = mat[rows, aligned(me3, nk)]
        mat_par = mat[rows, aligned(peer3, nk)]
        contract = (((1,), (1,)), ((), ()))
        part = 8

        @pl.loop(0, ni // part)
        def _(b):
            sel = pl.ds(b * part, part)
            term = lax.dot_general(vown[sel].reshape(part * nj, nk), mat_own, contract, preferred_element_type=F32)
            term += lax.dot_general(vpar[sel].reshape(part * nj, nk), mat_par, contract, preferred_element_type=F32)
            put(sel, term.astype(BF16).astype(F32).reshape(part, nj, LANES))

    def load_field(stage, r):
        return [pltpu.make_async_copy(field(stage, r), vown, load_sem.at[2]),
                pltpu.make_async_copy(lin3.at[stage * rhs + r], vpar, load_sem.at[3])]

    def load_terms(stage, c):
        g = stage * chunks + c
        return [pltpu.make_async_copy(t1.at[g], v1, load_sem.at[0]), pltpu.make_async_copy(t2.at[g], v2, load_sem.at[1])]

    def total_a(r, h):
        c, lanes = r * halves + h, aligned(h, LANES)
        wait_back(0, c)
        run(load_terms(0, c) + load_field(0, r) + [pltpu.make_async_copy(d_ref.at[:, :, lanes], vd, load_sem.at[4])])

        def put(sel, term):
            acc = v1[sel].astype(F32) + v2[sel].astype(F32) + term
            vw[sel] = (vd[sel] * acc.astype(BF16).astype(F32)).astype(BF16)

        third(0, h, put)
        run([pltpu.make_async_copy(vw, w.at[r, :, :, lanes], store_sem.at[0])])

    def third_b(r, h):
        run(load_field(1, r))

        def put(sel, term):
            z_ref[r, sel, :, aligned(h, LANES)] = term

        third(1, h, put)

    def total_b(r, h):
        c = r * halves + h
        third_b(r, h)
        wait_back(1, c)
        run(load_terms(1, c))
        part = 8

        @pl.loop(0, ni // part)
        def _(b):
            sel = pl.ds(b * part, part)
            z_ref[r, sel, :, aligned(h, LANES)] = (v1[sel].astype(F32) + v2[sel].astype(F32)) + z_ref[r, sel, :, aligned(h, LANES)]

    def total_last(r, h):
        c, lanes = r * halves + h, pl.ds(h * LANES, LANES)
        third_b(r, h)
        part = 16

        @pl.loop(0, ni // part)
        def _(b):
            last1[pl.ds(b * part, part), aligned(me1, jc), :] = vout1[pl.ds(me1 * ni + b * part, part)]

        @pl.loop(0, ic // part)
        def _(b):
            last2[pl.ds(me2 * ic + b * part, part)] = vout2[pl.ds(b * part, part), aligned(me2, nj), :]

        def tile(i_block, cols, part):
            @pl.loop(0, ic // part)
            def _(b):
                sel = pl.ds(i_block * ic + b * part, part)
                z_ref[r, sel, cols, lanes] = (last1[sel, cols, :].astype(F32) + last2[sel, cols, :].astype(F32)) + z_ref[r, sel, cols, lanes]

        @pl.loop(0, rhs)
        def _(e):
            wait_out_sends(0, e)
            wait_out_sends(1, e)

        @pl.loop(0, chunks)
        def _(e):
            wait_back_sends(0, e)

        @pl.loop(0, chunks - 1)
        def _(e):
            wait_back_sends(1, e)

        j_blocks = [me1] + [peer1[n1 - 2 - n] for n in order1]
        i_blocks = [me2] + [peer2[n2 - 2 - n] for n in order2]
        for m in range(max(n1, n2)):
            if m < n1:
                if m > 0:
                    back_y(1, c, order1[m - 1]).wait_recv()
                for e in range(min(m, n2)):
                    tile(i_blocks[e], aligned(j_blocks[m], jc), part)
            if m < n2:
                if m > 0:
                    back_x(1, c, order2[m - 1]).wait_recv()
                if m + 1 >= n1:
                    tile(i_blocks[m], slice(None), part // 2)
                else:
                    for e in range(m + 1):
                        tile(i_blocks[m], aligned(j_blocks[e], jc), part)
        wait_back_sends(1, c)

    @pl.loop(0, rhs)
    def _(r):
        start_out(0, r)

    run([pltpu.make_async_copy(src, dst, mat_sem.at[m]) for m, (src, dst) in enumerate(
        zip((a1_ref, a2_ref, a3_ref, b1_ref, b2_ref, b3_ref), (ma1, ma2, ma3, mb1, mb2, mb3)))])

    @pl.loop(0, rhs)
    def _(r):
        wait_out(0, r)

        @pl.loop(0, halves)
        def _(h):
            products(0, r, h)

    @pl.loop(0, rhs)
    def _(r):
        out_c(0, r).wait_recv()

        @pl.loop(0, halves)
        def _(h):
            total_a(r, h)

        start_out(1, r)

    @pl.loop(0, rhs - 1)
    def _(r):
        wait_out(1, r)

        @pl.loop(0, halves)
        def _(h):
            products(1, r, h)

    wait_out(1, rhs - 1)

    @pl.loop(0, halves - 1)
    def _(h):
        products(1, rhs - 1, h)

    products(1, rhs - 1, halves - 1)

    @pl.loop(0, rhs)
    def _(r):
        out_c(1, r).wait_recv()

    @pl.loop(0, chunks - 1)
    def _(c):
        total_b(c // halves, lax.rem(c, halves))

    total_last(rhs - 1, halves - 1)


def write_out(z_in, z_out, sem):
    rhs, parts = sem.shape
    size = z_in.shape[1] // parts
    copies = [pltpu.make_async_copy(z_in.at[r, pl.ds(b * size, size)], z_out.at[r, pl.ds(b * size, size)], sem.at[r, b])
              for r in range(rhs) for b in range(parts)]
    for copy in copies:
        copy.start()
    for copy in copies:
        copy.wait()


def solution(mesh):
    n1, n2, n3 = mesh.shape['mode1'], mesh.shape['mode2'], mesh.shape['mode3']
    vol_spec = P('rhs', 'mode1', 'mode2', 'mode3')
    diag_spec = P('mode1', 'mode2', 'mode3')

    def local_op(x_vol, diag_vals, *mats):
        rhs, ni, nj, nk = x_vol.shape
        dims = (n1, n2, n3, rhs, ni, nj, nk)
        halves = nk // LANES
        chunks = rhs * halves
        jc, ic = nj // n1, ni // n2
        hbm = pl.BlockSpec(memory_space=pltpu.HBM)
        vmem = pl.BlockSpec(memory_space=pltpu.VMEM)
        dma = pltpu.SemaphoreType.DMA
        block = (ni, nj, LANES)
        outs = [
            pltpu.VMEM(x_vol.shape, F32),
            jax.ShapeDtypeStruct((2 * rhs, n1 * ni, jc, nk), BF16),
            jax.ShapeDtypeStruct((2 * rhs, ic, n2 * nj, nk), BF16),
            jax.ShapeDtypeStruct((2 * rhs, ni, nj, nk), BF16),
            jax.ShapeDtypeStruct((2 * chunks, n1 * ni, jc, LANES), BF16),
            jax.ShapeDtypeStruct((2 * chunks, ic, n2 * nj, LANES), BF16),
            jax.ShapeDtypeStruct((2 * chunks,) + block, BF16),
            jax.ShapeDtypeStruct((2 * chunks,) + block, BF16),
            jax.ShapeDtypeStruct(x_vol.shape, BF16),
        ]
        scratch = [pltpu.VMEM(mat.shape, mat.dtype) for mat in mats] + [
            pltpu.VMEM((n1 * ni, jc, LANES), BF16),
            pltpu.VMEM((n1 * ni * jc, LANES), F32),
            pltpu.VMEM((n1 * ni, jc, LANES), BF16),
            pltpu.VMEM((ic, n2 * nj, LANES), BF16),
            pltpu.VMEM((ic, n2 * nj, LANES), BF16),
            pltpu.VMEM(block, BF16),
            pltpu.VMEM(block, BF16),
            pltpu.VMEM((ni, nj, nk), BF16),
            pltpu.VMEM((ni, nj, nk), BF16),
            pltpu.VMEM(block, F32),
            pltpu.VMEM(block, BF16),
            pltpu.VMEM(block, BF16),
            pltpu.VMEM(block, BF16),
            dma((2 * rhs, n1 - 1)), dma((2 * rhs, n1 - 1)),
            dma((2 * rhs, n2 - 1)), dma((2 * rhs, n2 - 1)),
            dma((2 * rhs,)), dma((2 * rhs,)),
            dma((2 * chunks, n1 - 1)), dma((2 * chunks, n1 - 1)),
            dma((2 * chunks, n2 - 1)), dma((2 * chunks, n2 - 1)),
            dma((len(mats),)), dma((max(5, n1, n2),)), dma((max(n1, n2),)),
        ]
        z_vol = pl.pallas_call(
            functools.partial(kernel, dims),
            out_shape=outs,
            in_specs=[hbm] * (2 + len(mats)),
            out_specs=[vmem] + [hbm] * (len(outs) - 1),
            scratch_shapes=scratch,
            compiler_params=pltpu.CompilerParams(collective_id=0, has_side_effects=True, vmem_limit_bytes=46 * 2 ** 20),
        )(x_vol, diag_vals, *mats)[0]
        return pl.pallas_call(
            write_out,
            out_shape=jax.ShapeDtypeStruct(x_vol.shape, F32),
            in_specs=[vmem],
            out_specs=hbm,
            scratch_shapes=[dma((rhs, 8))],
            compiler_params=pltpu.CompilerParams(vmem_limit_bytes=24 * 2 ** 20),
        )(z_vol)

    return jax.shard_map(local_op, mesh=mesh, in_specs=(vol_spec, diag_spec, P(), P(), P(), P(), P(), P()), out_specs=vol_spec, check_vma=False)
```

time: 1080 us -> 377 us (0.35)
  waiting for transfers between devices: 449 us -> 0 us
  Pallas kernels: 0 us -> 376 us
  local copies, waits for them, and re-layouts: 363 us -> 0 us
  other arithmetic: 85.5 us -> 0 us
  blocking collectives: 65.6 us -> 0 us
  matrix products: 58.8 us -> 0 us
  starting transfers between devices: 47.2 us -> 0 us
    all_to_all x8 -> x0, waiting for transfers between devices: 449 us -> none  [the longest x2 171 us: mode_sum(): whole_one = lax.all_to_all(volume, 'mode1', 2, 1, tiled=True)]
    pallas_call x0 -> x2, Pallas kernels: none -> 376 us  [the longest x1 370 us: local_op(): pl.pallas_call(functools.partial(kernel, dims), out_shape=outs, in_specs=...]
    convert_element_type x14 -> x0, local copies, waits for them, and re-layouts: 186 us -> none  [the longest x2 37 us: mode_sum(): term_three.astype(jnp.float32)]
    all_to_all x14 -> x0, local copies, waits for them, and re-layouts: 156 us -> none  [the longest x4 53.6 us: mode_sum(): whole_one = lax.all_to_all(volume, 'mode1', 2, 1, tiled=True)]
    convert_element_type x5 -> x0, other arithmetic: 68.4 us -> none  [the longest x2 23.6 us: mode_sum(): term_two.astype(jnp.float32)]
    all_to_all x4 -> x0, blocking collectives: 65.6 us -> none  [the longest x2 36.4 us: mode_sum(): term_three = lax.all_to_all(part_three, 'mode3', 3, 2, tiled=True)]
    dot_general x6 -> x0, matrix products: 58.8 us -> none  [the longest x2 20.4 us: mode_sum(): jnp.einsum('rijc,kc->rijk', whole_three, mat_three, preferred_element_typ...]
    all_to_all x8 -> x0, starting transfers between devices: 47.2 us -> none  [the longest x2 12.5 us: mode_sum(): whole_two = lax.all_to_all(volume, 'mode2', 1, 2, tiled=True)]
  transfers between devices with their start and end apart: 8 -> 0, of which waited for: 8 -> 0; matrix products, arithmetic and copies ran while one was open for 24% -> 0% of each run, Pallas kernels for 0% -> 0%
where the time goes in v4:
time: 377 us; the launch traced here: 376 us
  Pallas kernels  376 us (100%)
    pallas_call x1, Pallas kernels, local_op(): pl.pallas_call(functools.partial(kernel, dims), out_shape=outs, in_specs=...  370 us

profile of v4, /device:TPU:97, one launch (start us, length us, event | category | flops | bytes accessed | tf_op | source)
XLA Modules:
  0.0 376.1 jit_solution(17611099551794748659)
XLA Ops:
  0.0 370.1 %shard_map.82 = (f32[2,128,64,256]{3,2,1,0:T(8,128)S(1)}, bf16[4,512,16,256]{3,2,1,0:T(8,128)(2,1)}, bf16[4,32,256,256]{3,2,1,0:T(8,128)(2,1)}, bf16[4,128,64,25...) custom-call(bf16[2,128,64,256]{3,2,1,0:T(8,128)(2,1)} %x_ref.1, ...), custom_call_target="tpu_custom_call" | custom-call | tf_op jit(solution)/shard_map/pallas_call | solution.py:392
  370.1 6.0 %shard_map.83 = f32[2,128,64,256]{3,2,1,0:T(8,128)} custom-call(f32[2,128,64,256]{3,2,1,0:T(8,128)S(1)} %get-tuple-element.6.z_in), custom_call_target="tpu_custom_call" | custom-call | tf_op jit(solution)/shard_map/pallas_call | solution.py:400

commit v5 on v4

--- a/solution.py
+++ b/solution.py
@@ -24,7 +24,6 @@
            y_send2, y_recv2, x_send2, x_recv2, mat_sem, load_sem, store_sem):
     n1, n2, n3, rhs, ni, nj, nk = dims
     halves = nk // LANES
-    chunks = rhs * halves
     jc, ic = nj // n1, ni // n2
     me1, me2, me3 = lax.axis_index('mode1'), lax.axis_index('mode2'), lax.axis_index('mode3')
     peer1 = [lax.rem(me1 + s, n1) for s in range(1, n1)]
@@ -67,20 +66,28 @@
         q = stage * rhs + r
         return remote(field(stage, r), lin3.at[q], c_send.at[q], c_recv.at[q], 'mode3', peer3)
 
-    def is_last(stage, c):
-        return stage == 1 and isinstance(c, int) and c == chunks - 1
-
-    def back_y(stage, c, n):
-        g = stage * chunks + c
-        dst = last1 if is_last(stage, c) else t1.at[g]
-        return remote(out1.at[g, aligned(peer1[n], ni)], dst.at[:, aligned(me1, jc), :],
-                      y_send2.at[g, n], y_recv2.at[g, n], 'mode1', peer1[n])
-
-    def back_x(stage, c, n):
-        g = stage * chunks + c
-        dst = last2 if is_last(stage, c) else t2.at[g]
-        return remote(out2.at[g, :, aligned(peer2[n], nj), :], dst.at[aligned(me2, ic)],
-                      x_send2.at[g, n], x_recv2.at[g, n], 'mode2', peer2[n])
+    def back_y(stage, r, n, h=None):
+        q = stage * rhs + r
+        row, lanes = (q, slice(None)) if h is None else (2 * rhs - 1 + h, aligned(h, LANES))
+        dst = last1 if is_last(h) else t1.at[q, :, :, lanes]
+        return remote(out1.at[q, aligned(peer1[n], ni), :, lanes], dst.at[:, aligned(me1, jc), :],
+                      y_send2.at[row, n], y_recv2.at[row, n], 'mode1', peer1[n])
+
+    def back_x(stage, r, n, h=None):
+        q = stage * rhs + r
+        row, lanes = (q, slice(None)) if h is None else (2 * rhs - 1 + h, aligned(h, LANES))
+        dst = last2 if is_last(h) else t2.at[q, :, :, lanes]
+        return remote(out2.at[q, :, aligned(peer2[n], nj), lanes], dst.at[aligned(me2, ic)],
+                      x_send2.at[row, n], x_recv2.at[row, n], 'mode2', peer2[n])
+
+    def is_last(h):
+        return isinstance(h, int) and h == halves - 1
+
+    def start_back(stage, r, h=None):
+        for n in order1:
+            back_y(stage, r, n, h).start()
+        for n in order2:
+            back_x(stage, r, n, h).start()
 
     def start_out(stage, r):
         for n in order1:
@@ -95,11 +102,11 @@
         for n in range(n2 - 1):
             out_x(stage, r, n).wait_recv()
 
-    def wait_back(stage, c):
+    def wait_back(stage, r, h=None):
         for n in range(n1 - 1):
-            back_y(stage, c, n).wait_recv()
+            back_y(stage, r, n, h).wait_recv()
         for n in range(n2 - 1):
-            back_x(stage, c, n).wait_recv()
+            back_x(stage, r, n, h).wait_recv()
 
     def wait_out_sends(stage, r):
         for n in range(n1 - 1):
@@ -108,14 +115,14 @@
             out_x(stage, r, n).wait_send()
         out_c(stage, r).wait_send()
 
-    def wait_back_sends(stage, c):
+    def wait_back_sends(stage, r, h=None):
         for n in range(n1 - 1):
-            back_y(stage, c, n).wait_send()
+            back_y(stage, r, n, h).wait_send()
         for n in range(n2 - 1):
-            back_x(stage, c, n).wait_send()
-
-    def product_one(stage, r, h, c):
-        q, g, lanes = stage * rhs + r, stage * chunks + c, aligned(h, LANES)
+            back_x(stage, r, n, h).wait_send()
+
+    def product_one(stage, r, h, last):
+        q, lanes = stage * rhs + r, aligned(h, LANES)
         mat = (ma1, mb1)[stage]
         run([pltpu.make_async_copy(field(stage, r).at[:, aligned(me1, jc), lanes], vin1.at[aligned(me1, ni)], load_sem.at[0])]
             + [pltpu.make_async_copy(lin1.at[q, aligned(peer1[n], ni), :, lanes], vin1.at[aligned(peer1[n], ni)], load_sem.at[n + 1])
@@ -139,16 +146,14 @@
         def _(b):
             vout1[pl.ds(b * part, part)] = vscr[aligned(b, part * jc), :].reshape(part, jc, LANES).astype(BF16)
 
-        stores = [pltpu.make_async_copy(vout1.at[aligned(peer1[n], ni)], out1.at[g, aligned(peer1[n], ni)], store_sem.at[n + 1])
+        stores = [pltpu.make_async_copy(vout1.at[aligned(peer1[n], ni)], out1.at[q, aligned(peer1[n], ni), :, lanes], store_sem.at[n + 1])
                   for n in range(n1 - 1)]
-        if not is_last(stage, c):
-            stores += [pltpu.make_async_copy(vout1.at[aligned(me1, ni)], t1.at[g, :, aligned(me1, jc), :], store_sem.at[0])]
+        if not last:
+            stores += [pltpu.make_async_copy(vout1.at[aligned(me1, ni)], t1.at[q, :, aligned(me1, jc), lanes], store_sem.at[0])]
         run(stores)
-        for n in order1:
-            back_y(stage, c, n).start()
-
-    def product_two(stage, r, h, c):
-        q, g, lanes = stage * rhs + r, stage * chunks + c, aligned(h, LANES)
+
+    def product_two(stage, r, h, last):
+        q, lanes = stage * rhs + r, aligned(h, LANES)
         mat = (ma2, mb2)[stage]
         run([pltpu.make_async_copy(field(stage, r).at[aligned(me2, ic), :, lanes], vin2.at[:, aligned(me2, nj), :], load_sem.at[0])]
             + [pltpu.make_async_copy(lin2.at[q, :, aligned(peer2[n], nj), lanes], vin2.at[:, aligned(peer2[n], nj), :], load_sem.at[n + 1])
@@ -161,18 +166,15 @@
             vout2[2 * b] = res[:, :LANES]
             vout2[2 * b + 1] = res[:, LANES:]
 
-        stores = [pltpu.make_async_copy(vout2.at[:, aligned(peer2[n], nj), :], out2.at[g, :, aligned(peer2[n], nj), :], store_sem.at[n + 1])
+        stores = [pltpu.make_async_copy(vout2.at[:, aligned(peer2[n], nj), :], out2.at[q, :, aligned(peer2[n], nj), lanes], store_sem.at[n + 1])
                   for n in range(n2 - 1)]
-        if not is_last(stage, c):
-            stores += [pltpu.make_async_copy(vout2.at[:, aligned(me2, nj), :], t2.at[g, aligned(me2, ic)], store_sem.at[0])]
+        if not last:
+            stores += [pltpu.make_async_copy(vout2.at[:, aligned(me2, nj), :], t2.at[q, aligned(me2, ic), :, lanes], store_sem.at[0])]
         run(stores)
-        for n in order2:
-            back_x(stage, c, n).start()
-
-    def products(stage, r, h):
-        c = r * halves + h
-        product_one(stage, r, h, c)
-        product_two(stage, r, h, c)
+
+    def products(stage, r, h, last=False):
+        product_one(stage, r, h, last)
+        product_two(stage, r, h, last)
 
     def third(stage, h, put):
         mat = (ma3, mb3)[stage]
@@ -193,14 +195,13 @@
         return [pltpu.make_async_copy(field(stage, r), vown, load_sem.at[2]),
                 pltpu.make_async_copy(lin3.at[stage * rhs + r], vpar, load_sem.at[3])]
 
-    def load_terms(stage, c):
-        g = stage * chunks + c
-        return [pltpu.make_async_copy(t1.at[g], v1, load_sem.at[0]), pltpu.make_async_copy(t2.at[g], v2, load_sem.at[1])]
+    def load_terms(stage, r, h):
+        q, lanes = stage * rhs + r, aligned(h, LANES)
+        return [pltpu.make_async_copy(t1.at[q, :, :, lanes], v1, load_sem.at[0]), pltpu.make_async_copy(t2.at[q, :, :, lanes], v2, load_sem.at[1])]
 
     def total_a(r, h):
-        c, lanes = r * halves + h, aligned(h, LANES)
-        wait_back(0, c)
-        run(load_terms(0, c) + load_field(0, r) + [pltpu.make_async_copy(d_ref.at[:, :, lanes], vd, load_sem.at[4])])
+        lanes = aligned(h, LANES)
+        run(load_terms(0, r, h) + load_field(0, r) + [pltpu.make_async_copy(d_ref.at[:, :, lanes], vd, load_sem.at[4])])
 
         def put(sel, term):
             acc = v1[sel].astype(F32) + v2[sel].astype(F32) + term
@@ -218,10 +219,7 @@
         third(1, h, put)
 
     def total_b(r, h):
-        c = r * halves + h
-        third_b(r, h)
-        wait_back(1, c)
-        run(load_terms(1, c))
+        run(load_terms(1, r, h))
         part = 8
 
         @pl.loop(0, ni // part)
@@ -230,7 +228,7 @@
             z_ref[r, sel, :, aligned(h, LANES)] = (v1[sel].astype(F32) + v2[sel].astype(F32)) + z_ref[r, sel, :, aligned(h, LANES)]
 
     def total_last(r, h):
-        c, lanes = r * halves + h, pl.ds(h * LANES, LANES)
+        lanes = pl.ds(h * LANES, LANES)
         third_b(r, h)
         part = 16
 
@@ -252,32 +250,33 @@
         def _(e):
             wait_out_sends(0, e)
             wait_out_sends(1, e)
-
-        @pl.loop(0, chunks)
-        def _(e):
             wait_back_sends(0, e)
 
-        @pl.loop(0, chunks - 1)
+        @pl.loop(0, rhs - 1)
         def _(e):
             wait_back_sends(1, e)
+
+        @pl.loop(0, halves - 1)
+        def _(e):
+            wait_back_sends(1, r, e)
 
         j_blocks = [me1] + [peer1[n1 - 2 - n] for n in order1]
         i_blocks = [me2] + [peer2[n2 - 2 - n] for n in order2]
         for m in range(max(n1, n2)):
             if m < n1:
                 if m > 0:
-                    back_y(1, c, order1[m - 1]).wait_recv()
+                    back_y(1, r, order1[m - 1], h).wait_recv()
                 for e in range(min(m, n2)):
                     tile(i_blocks[e], aligned(j_blocks[m], jc), part)
             if m < n2:
                 if m > 0:
-                    back_x(1, c, order2[m - 1]).wait_recv()
+                    back_x(1, r, order2[m - 1], h).wait_recv()
                 if m + 1 >= n1:
                     tile(i_blocks[m], slice(None), part // 2)
                 else:
                     for e in range(m + 1):
                         tile(i_blocks[m], aligned(j_blocks[e], jc), part)
-        wait_back_sends(1, c)
+        wait_back_sends(1, r, h)
 
     @pl.loop(0, rhs)
     def _(r):
@@ -294,9 +293,12 @@
         def _(h):
             products(0, r, h)
 
+        start_back(0, r)
+
     @pl.loop(0, rhs)
     def _(r):
         out_c(0, r).wait_recv()
+        wait_back(0, r)
 
         @pl.loop(0, halves)
         def _(h):
@@ -312,23 +314,42 @@
         def _(h):
             products(1, r, h)
 
-    wait_out(1, rhs - 1)
+        start_back(1, r)
+
+    end = rhs - 1
+    wait_out(1, end)
 
     @pl.loop(0, halves - 1)
     def _(h):
-        products(1, rhs - 1, h)
-
-    products(1, rhs - 1, halves - 1)
+        products(1, end, h)
+        start_back(1, end, h)
+
+    products(1, end, halves - 1, True)
+    start_back(1, end, halves - 1)
 
     @pl.loop(0, rhs)
     def _(r):
         out_c(1, r).wait_recv()
 
-    @pl.loop(0, chunks - 1)
-    def _(c):
-        total_b(c // halves, lax.rem(c, halves))
-
-    total_last(rhs - 1, halves - 1)
+    @pl.loop(0, rhs - 1)
+    def _(r):
+        @pl.loop(0, halves)
+        def _(h):
+            third_b(r, h)
+
+        wait_back(1, r)
+
+        @pl.loop(0, halves)
+        def _(h):
+            total_b(r, h)
+
+    @pl.loop(0, halves - 1)
+    def _(h):
+        third_b(end, h)
+        wait_back(1, end, h)
+        total_b(end, h)
+
+    total_last(end, halves - 1)
 
 
 def write_out(z_in, z_out, sem):
@@ -351,7 +372,7 @@
         rhs, ni, nj, nk = x_vol.shape
         dims = (n1, n2, n3, rhs, ni, nj, nk)
         halves = nk // LANES
-        chunks = rhs * halves
+        backs = 2 * rhs - 1 + halves
         jc, ic = nj // n1, ni // n2
         hbm = pl.BlockSpec(memory_space=pltpu.HBM)
         vmem = pl.BlockSpec(memory_space=pltpu.VMEM)
@@ -362,10 +383,10 @@
             jax.ShapeDtypeStruct((2 * rhs, n1 * ni, jc, nk), BF16),
             jax.ShapeDtypeStruct((2 * rhs, ic, n2 * nj, nk), BF16),
             jax.ShapeDtypeStruct((2 * rhs, ni, nj, nk), BF16),
-            jax.ShapeDtypeStruct((2 * chunks, n1 * ni, jc, LANES), BF16),
-            jax.ShapeDtypeStruct((2 * chunks, ic, n2 * nj, LANES), BF16),
-            jax.ShapeDtypeStruct((2 * chunks,) + block, BF16),
-            jax.ShapeDtypeStruct((2 * chunks,) + block, BF16),
+            jax.ShapeDtypeStruct((2 * rhs, n1 * ni, jc, nk), BF16),
+            jax.ShapeDtypeStruct((2 * rhs, ic, n2 * nj, nk), BF16),
+            jax.ShapeDtypeStruct((2 * rhs, ni, nj, nk), BF16),
+            jax.ShapeDtypeStruct((2 * rhs, ni, nj, nk), BF16),
             jax.ShapeDtypeStruct(x_vol.shape, BF16),
         ]
         scratch = [pltpu.VMEM(mat.shape, mat.dtype) for mat in mats] + [
@@ -385,8 +406,8 @@
             dma((2 * rhs, n1 - 1)), dma((2 * rhs, n1 - 1)),
             dma((2 * rhs, n2 - 1)), dma((2 * rhs, n2 - 1)),
             dma((2 * rhs,)), dma((2 * rhs,)),
-            dma((2 * chunks, n1 - 1)), dma((2 * chunks, n1 - 1)),
-            dma((2 * chunks, n2 - 1)), dma((2 * chunks, n2 - 1)),
+            dma((backs, n1 - 1)), dma((backs, n1 - 1)),
+            dma((backs, n2 - 1)), dma((backs, n2 - 1)),
             dma((len(mats),)), dma((max(5, n1, n2),)), dma((max(n1, n2),)),
         ]
         z_vol = pl.pallas_call(
@@ -402,7 +423,7 @@
             out_shape=jax.ShapeDtypeStruct(x_vol.shape, F32),
             in_specs=[vmem],
             out_specs=hbm,
-            scratch_shapes=[dma((rhs, 8))],
+            scratch_shapes=[dma((rhs, 4))],
             compiler_params=pltpu.CompilerParams(vmem_limit_bytes=24 * 2 ** 20),
         )(z_vol)
 

time: 377 us -> 376 us (level)
  no operation moved by 1% of the time
where the time goes in v5:
time: 376 us
  Pallas kernels  376 us (100%)
    pallas_call x1, Pallas kernels, local_op(): pl.pallas_call(functools.partial(kernel, dims), out_shape=outs, in_specs=...  370 us

profile of v5, /device:TPU:97, one launch (start us, length us, event | category | flops | bytes accessed | tf_op | source)
XLA Modules:
  0.0 375.7 jit_solution(8006437696985542795)
XLA Ops:
  0.0 369.7 %shard_map.82 = (f32[2,128,64,256]{3,2,1,0:T(8,128)S(1)}, bf16[4,512,16,256]{3,2,1,0:T(8,128)(2,1)}, bf16[4,32,256,256]{3,2,1,0:T(8,128)(2,1)}, bf16[4,128,64,25...) custom-call(bf16[2,128,64,256]{3,2,1,0:T(8,128)(2,1)} %x_ref.1, ...), custom_call_target="tpu_custom_call" | custom-call | tf_op jit(solution)/shard_map/pallas_call | solution.py:413
  369.7 5.9 %shard_map.83 = f32[2,128,64,256]{3,2,1,0:T(8,128)} custom-call(f32[2,128,64,256]{3,2,1,0:T(8,128)S(1)} %get-tuple-element.6.z_in), custom_call_target="tpu_custom_call" | custom-call | tf_op jit(solution)/shard_map/pallas_call | solution.py:421

commit v6 on v5

--- a/solution.py
+++ b/solution.py
@@ -83,9 +83,11 @@
     def is_last(h):
         return isinstance(h, int) and h == halves - 1
 
-    def start_back(stage, r, h=None):
+    def start_back_y(stage, r, h=None):
         for n in order1:
             back_y(stage, r, n, h).start()
+
+    def start_back_x(stage, r, h=None):
         for n in order2:
             back_x(stage, r, n, h).start()
 
@@ -96,9 +98,11 @@
             out_x(stage, r, n).start()
         out_c(stage, r).start()
 
-    def wait_out(stage, r):
+    def wait_out_y(stage, r):
         for n in range(n1 - 1):
             out_y(stage, r, n).wait_recv()
+
+    def wait_out_x(stage, r):
         for n in range(n2 - 1):
             out_x(stage, r, n).wait_recv()
 
@@ -172,9 +176,21 @@
             stores += [pltpu.make_async_copy(vout2.at[:, aligned(me2, nj), :], t2.at[q, aligned(me2, ic), :, lanes], store_sem.at[0])]
         run(stores)
 
-    def products(stage, r, h, last=False):
-        product_one(stage, r, h, last)
-        product_two(stage, r, h, last)
+    def products(stage, r):
+        wait_out_y(stage, r)
+
+        @pl.loop(0, halves)
+        def _(h):
+            product_one(stage, r, h, False)
+
+        start_back_y(stage, r)
+        wait_out_x(stage, r)
+
+        @pl.loop(0, halves)
+        def _(h):
+            product_two(stage, r, h, False)
+
+        start_back_x(stage, r)
 
     def third(stage, h, put):
         mat = (ma3, mb3)[stage]
@@ -287,13 +303,7 @@
 
     @pl.loop(0, rhs)
     def _(r):
-        wait_out(0, r)
-
-        @pl.loop(0, halves)
-        def _(h):
-            products(0, r, h)
-
-        start_back(0, r)
+        products(0, r)
 
     @pl.loop(0, rhs)
     def _(r):
@@ -308,24 +318,23 @@
 
     @pl.loop(0, rhs - 1)
     def _(r):
-        wait_out(1, r)
-
-        @pl.loop(0, halves)
-        def _(h):
-            products(1, r, h)
-
-        start_back(1, r)
+        products(1, r)
 
     end = rhs - 1
-    wait_out(1, end)
+    wait_out_y(1, end)
+    wait_out_x(1, end)
 
     @pl.loop(0, halves - 1)
     def _(h):
-        products(1, end, h)
-        start_back(1, end, h)
-
-    products(1, end, halves - 1, True)
-    start_back(1, end, halves - 1)
+        product_one(1, end, h, False)
+        start_back_y(1, end, h)
+        product_two(1, end, h, False)
+        start_back_x(1, end, h)
+
+    product_one(1, end, halves - 1, True)
+    start_back_y(1, end, halves - 1)
+    product_two(1, end, halves - 1, True)
+    start_back_x(1, end, halves - 1)
 
     @pl.loop(0, rhs)
     def _(r):

time: 376 us -> 376 us (level)
  no operation moved by 1% of the time
where the time goes in v6:
time: 376 us
  Pallas kernels  376 us (100%)
    pallas_call x1, Pallas kernels, local_op(): pl.pallas_call(functools.partial(kernel, dims), out_shape=outs, in_specs=...  370 us

profile of v6, /device:TPU:97, one launch (start us, length us, event | category | flops | bytes accessed | tf_op | source)
XLA Modules:
  0.0 375.7 jit_solution(9937420665870816384)
XLA Ops:
  0.0 369.7 %shard_map.82 = (f32[2,128,64,256]{3,2,1,0:T(8,128)S(1)}, bf16[4,512,16,256]{3,2,1,0:T(8,128)(2,1)}, bf16[4,32,256,256]{3,2,1,0:T(8,128)(2,1)}, bf16[4,128,64,25...) custom-call(bf16[2,128,64,256]{3,2,1,0:T(8,128)(2,1)} %x_ref.1, ...), custom_call_target="tpu_custom_call" | custom-call | tf_op jit(solution)/shard_map/pallas_call | solution.py:422
  369.7 5.9 %shard_map.83 = f32[2,128,64,256]{3,2,1,0:T(8,128)} custom-call(f32[2,128,64,256]{3,2,1,0:T(8,128)S(1)} %get-tuple-element.6.z_in), custom_call_target="tpu_custom_call" | custom-call | tf_op jit(solution)/shard_map/pallas_call | solution.py:430
